TPU v7x, 16 devices: a whole 2x2x2 slice. The times are simulated.
16 devices in a mesh: replica: 2 (over z), data: 8 (over y, x, core).
Axes of the slice: x: 2, y: 2, z: 2, core: 2. Of those that a mesh axis runs over, the one named last changes fastest.
Arguments:
- x: bfloat16 [8192, 3072], P(('replica', 'data')), parts along dimension 0
- adapter_id: int32 [8192], P(('replica', 'data')), parts along dimension 0
- w_gate: bfloat16 [3072, 8192], replicated
- w_up: bfloat16 [3072, 8192], replicated
- w_down: bfloat16 [8192, 3072], replicated
- a_gate: bfloat16 [64, 3072, 64], P('data')
- b_gate: bfloat16 [64, 64, 8192], P('data')
- a_up: bfloat16 [64, 3072, 64], P('data')
- b_up: bfloat16 [64, 64, 8192], P('data')
- a_down: bfloat16 [64, 8192, 64], P('data')
- b_down: bfloat16 [64, 64, 3072], P('data')
- hot_ids: int32 [4], replicated
- hot_a_gate: bfloat16 [4, 3072, 64], replicated
- hot_b_gate: bfloat16 [4, 64, 8192], replicated
- hot_a_up: bfloat16 [4, 3072, 64], replicated
- hot_b_up: bfloat16 [4, 64, 8192], replicated
- hot_a_down: bfloat16 [4, 8192, 64], replicated
- hot_b_down: bfloat16 [4, 64, 3072], replicated
Outputs:
- output: bfloat16 [8192, 3072], P(('replica', 'data')), parts along dimension 0
There are 2 independent parts. A program takes and returns all parts, laid end to end along the dimension named above; an argument that names none is the same for every part.
All inputs are finite; a program needn't handle non-finite values.
Results may differ from a plain program's by a relative error of at most 0.00144.
Values are sent between devices in bfloat16 or wider.
A program may use at most 1 GiB of HBM per device.

v0:
```python
import jax
import jax.numpy as jnp
from jax import lax
from jax.sharding import PartitionSpec as P

value_a10 = 32


def route_layout(tok_ids, hot_ids, group_size, n_local, capacity):
    tok_count = tok_ids.shape[0]
    hot_match = tok_ids[:, None] == hot_ids[None, :]
    is_hot = jnp.any(hot_match, axis=1)
    owner_of = jnp.where(is_hot, group_size, tok_ids // n_local)
    sort_order = jnp.argsort(owner_of, stable=True)
    counts = jax.ops.segment_sum(jnp.ones_like(owner_of), owner_of, num_segments=group_size + 1)
    starts = jnp.cumsum(counts) - counts
    within = jnp.arange(capacity)
    slot_tok = sort_order[jnp.minimum(starts[:group_size, None] + within[None, :], tok_count - 1)].reshape(-1)
    slot_ok = (within[None, :] < counts[:group_size, None]).reshape(-1)
    sort_rank = jnp.zeros_like(owner_of).at[sort_order].set(jnp.arange(tok_count, dtype=owner_of.dtype))
    owner_safe = jnp.minimum(owner_of, group_size - 1)
    tok_slot = owner_safe * capacity + jnp.clip(sort_rank - starts[owner_safe], 0, capacity - 1)
    return hot_match.astype(jnp.bfloat16), is_hot, slot_tok, slot_ok, tok_slot


def adapter_delta(tok_rows, select, a_set, b_set, array_b10):
    low_rank = jnp.einsum("md,ndr->mnr", tok_rows, a_set, preferred_element_type=jnp.float32).astype(jnp.bfloat16)
    low_rank = low_rank * select[:, :, None]
    delta_f = jnp.einsum("mnr,nrf->mf", low_rank, b_set, preferred_element_type=jnp.float32)
    return (array_b10 * delta_f).astype(jnp.bfloat16)


def solution(mesh):
    group_size = mesh.shape["data"]
    token_spec = P(("replica", "data"), None)
    store_spec = P("data", None, None)
    full_mat = P(None, None)
    full_set = P(None, None, None)
    in_specs = (token_spec, P(("replica", "data")), full_mat, full_mat, full_mat) + (store_spec,) * 6 + (P(None),) + (full_set,) * 6

    def device_step(x, adapter_id, w_gate, w_up, w_down, a_gate, b_gate, a_up, b_up, a_down, b_down, hot_ids, hot_a_gate, hot_b_gate, hot_a_up, hot_b_up, hot_a_down, hot_b_down):
        tok_count = x.shape[0]
        n_local = a_gate.shape[0]
        array_b10 = value_a10 / a_gate.shape[2]
        capacity = tok_count // (2 * group_size)
        hot_sel, is_hot, slot_tok, slot_ok, tok_slot = route_layout(adapter_id, hot_ids, group_size, n_local, capacity)

        def exchange(send_rows):
            return lax.all_to_all(send_rows, "data", 0, 0, tiled=True)

        def to_tokens(back_rows):
            return jnp.where(is_hot[:, None], 0.0, jnp.take(back_rows, tok_slot, axis=0).astype(jnp.float32))

        send_ids = jnp.where(slot_ok, jnp.take(adapter_id, slot_tok), -1)
        recv_ids = exchange(send_ids) - lax.axis_index("data") * n_local
        owner_sel = (recv_ids[:, None] == jnp.arange(n_local)[None, :]).astype(jnp.bfloat16)

        recv_x = exchange(jnp.take(x, slot_tok, axis=0))
        gate_back = exchange(adapter_delta(recv_x, owner_sel, a_gate, b_gate, array_b10))
        up_back = exchange(adapter_delta(recv_x, owner_sel, a_up, b_up, array_b10))
        gate_act = (jnp.dot(x, w_gate, preferred_element_type=jnp.float32)
                    + adapter_delta(x, hot_sel, hot_a_gate, hot_b_gate, array_b10).astype(jnp.float32)
                    + to_tokens(gate_back))
        up_act = (jnp.dot(x, w_up, preferred_element_type=jnp.float32)
                  + adapter_delta(x, hot_sel, hot_a_up, hot_b_up, array_b10).astype(jnp.float32)
                  + to_tokens(up_back))
        hidden = (jax.nn.silu(gate_act) * up_act).astype(jnp.bfloat16)

        recv_h = exchange(jnp.take(hidden, slot_tok, axis=0))
        down_back = exchange(adapter_delta(recv_h, owner_sel, a_down, b_down, array_b10))
        down_out = (jnp.dot(hidden, w_down, preferred_element_type=jnp.float32)
                    + adapter_delta(hidden, hot_sel, hot_a_down, hot_b_down, array_b10).astype(jnp.float32)
                    + to_tokens(down_back))
        return (x.astype(jnp.float32) + down_out).astype(jnp.bfloat16)

    return jax.shard_map(device_step, mesh=mesh, in_specs=in_specs, out_specs=token_spec, check_vma=False)
```

profile of v0, /device:TPU:0, one launch (start us, length us, event | category | flops | bytes accessed | tf_op | source)
XLA Modules:
  0.0 378.8 jit_solution(3950242200549871915)
XLA Ops:
  0.0 0.9 compare_reduce_fusion
  0.9 0.7 fusion.29
  1.7 4.1 %scatter_custom_fusion = s32[9]{0:T(128)S(1)} fusion(s32[512]{0:T(512)S(1)} %fusion.29, s32[512]{0:T(512)S(1)} %ne.14, s32[]{:T(128)} %constant.67.clone.1), kind=kCustom, calls=%fused_computation.80 | custom fusion | flops 512 | bytes 40 | tf_op jit(solution)/shard_map/scatter-add | solution.py:15
  5.8 0.2 reduce-window.9
  6.0 3.8 sort.17
  9.7 0.1 compare_select_fusion.2
  9.8 0.1 reshape.284
  9.9 1.9 gather_fusion
  11.9 0.1 gather.36
  12.0 1.9 gather_fusion.2
  13.9 0.1 gather.38
  14.0 0.7 select_select_fusion
  14.7 5.5 %all-to-all-start.1 = ((s32[8,32,1]{1,2,0:T(1,128)}), s32[8,32,1]{1,2,0:T(1,128)S(1)}, u32[]{:S(2)}, u32[]{:S(2)}) async-start(s32[8,32,1]{1,2,0:T(1,128)} %bitcast.22), calls=%async_computation.1 | async-start | bytes 8192 | tf_op jit(solution)/shard_map/all_to_all | solution.py:49
  20.1 0.1 reshape.283
  20.2 6.6 %gather_fusion.1 = bf16[256,3072]{1,0:T(8,128)(2,1)} fusion(bf16[512,3072]{1,0:T(8,128)(2,1)} %param.20, s32[1024]{0:T(1024)S(1)} %pad_clamp_fusion.1), kind=kCustom, calls=%fused_computation.3 | custom fusion | bytes 3146752 | tf_op jit(solution)/shard_map/jit(_take)/gather | solution.py:58
  26.8 0.0 copy-done.13
  26.8 2.8 broadcast_select_fusion.1
  29.6 0.0 all-to-all-done.1
  29.6 4.3 %all-to-all-start = ((bf16[8,32,3072]{2,1,0:T(8,128)(2,1)}), bf16[8,32,3072]{2,1,0:T(8,128)(2,1)}, u32[]{:S(2)}, u32[]{:S(2)}) async-start(bf16[8,32,3072]{2,1,0:T(8,128)(2,1)} %broadcast_select_fusion.1), calls=%async_computation | async-start | bytes 3145728 | tf_op jit(solution)/shard_map/all_to_all | solution.py:49
  33.9 2.6 scatter_custom_fusion.1
  36.6 0.0 copy-start.3
  36.6 0.0 copy-start.17
  36.6 0.7 fusion.38
  37.3 4.5 %fusion.40 = f32[512,256]{0,1} fusion(bf16[512,3072]{1,0:T(8,128)(2,1)} %param.20, bf16[3072,256]{0,1:T(8,128)(2,1)} %bitcast.132), kind=kOutput, calls=%fused_computation.84 | convolution fusion | flops 805306368 | bytes 5242880
  41.8 1.9 fusion.42
  43.7 0.1 sub.29
  43.7 11.0 %all-to-all-done = bf16[8,32,3072]{2,1,0:T(8,128)(2,1)} async-done(((bf16[8,32,3072]{2,1,0:T(8,128)(2,1)}), bf16[8,32,3072]{2,1,0:T(8,128)(2,1)}, u32[]{:S(2)}, u32[]{:S(2)}) %all-to-all-start) | async-done | bytes 1572896 | tf_op jit(solution)/shard_map/all_to_all | solution.py:49
  54.8 2.4 fusion.41
  57.2 7.9 %fusion.4 = bf16[256,8192]{1,0:T(8,128)(2,1)} fusion(bf16[8,64,8192]{2,1,0:T(8,128)(2,1)} %param.26, f32[256,8,64]{0,2,1:T(8,128)S(1)} %bitcast.118, bf16[256,8]{0,1:T(8,128)(2,1)S(1)} %fusion.27), kind=kOutput, calls=%fused_computation.18 | convolution fusion | flops 2151940096 | bytes 13111296 | tf_op jit(solution)/shard_map/mnr,nrf->mf/dot_general | solution.py:29
  65.1 4.9 %all-to-all-start.2 = ((bf16[8,32,8192]{2,1,0:T(8,128)(2,1)}), bf16[8,32,8192]{2,1,0:T(8,128)(2,1)}, u32[]{:S(2)}, u32[]{:S(2)}) async-start(bf16[8,32,8192]{2,1,0:T(8,128)(2,1)} %bitcast.110), calls=%async_computation.2 | async-start | bytes 8388608 | tf_op jit(solution)/shard_map/all_to_all | solution.py:49
  70.0 5.7 %compare_and_fusion.1 = (pred[512]{0:T(512)(128)(4,1)S(1)}, s32[512]{0:T(512)S(1)}) fusion(s32[512]{0:T(512)S(1)} %scatter_custom_fusion.1, s32[]{:T(128)} %bitcast.14, s32[]{:T(128)} %bitcast.13, s32[]{:T(128)} %bitcast.12, s32[]{:T(128)} %bitcast.11, s32[]{:T(128)} %bitcast.10, s32[]{:T(128)} %bitcast.9, s32[]{:T(128)} %bitcast.8, s32[]{:T(128)} %bitcast.7, ...), kind=kLoop, calls=%fused_computation.75 | loop fusion | flops 15360 | bytes 6692 | tf_op jit(solution)/shard_map/jit(_take)/and | solution.py:52
  75.7 0.0 copy-done.10
  75.8 0.0 copy-start.5
  75.8 0.0 slice-start
  75.8 8.0 %fusion = bf16[512,8192]{1,0:T(8,128)(2,1)} fusion(bf16[4,64,8192]{2,1,0:T(8,128)(2,1)} %param.35, f32[512,4,64]{0,2,1:T(8,128)S(1)} %bitcast.120, bf16[512,4]{0,1:T(4,128)(2,1)S(1)} %get-tuple-element.11), kind=kOutput, calls=%fused_computation.10 | convolution fusion | flops 2156134400 | bytes 13111296 | tf_op jit(solution)/shard_map/mnr,nrf->mf/dot_general | solution.py:29
  83.8 0.0 copy-start.16
  83.8 0.0 slice-start.1
  83.8 5.6 %fusion.1 = bf16[512,8192]{1,0:T(8,128)(2,1)} fusion(bf16[4,64,8192]{2,1,0:T(8,128)(2,1)S(1)} %copy-done.5, f32[512,4,64]{0,2,1:T(8,128)S(1)} %bitcast.119, bf16[512,4]{0,1:T(4,128)(2,1)S(1)} %get-tuple-element.11), kind=kOutput, calls=%fused_computation.12 | convolution fusion | flops 2156134400 | bytes 13111296 | tf_op jit(solution)/shard_map/mnr,nrf->mf/dot_general | solution.py:29
  89.4 2.4 fusion.43
  91.9 4.4 %fusion.5 = bf16[256,8192]{1,0:T(8,128)(2,1)} fusion(bf16[8,64,8192]{2,1,0:T(8,128)(2,1)S(1)} %bitcast.114, f32[256,8,64]{0,2,1:T(8,128)S(1)} %bitcast.117, bf16[256,8]{0,1:T(8,128)(2,1)S(1)} %fusion.27), kind=kOutput, calls=%fused_computation.19 | convolution fusion | flops 2151940096 | bytes 13111296 | tf_op jit(solution)/shard_map/mnr,nrf->mf/dot_general | solution.py:29
  96.3 22.8 %all-to-all-done.2 = bf16[8,32,8192]{2,1,0:T(8,128)(2,1)} async-done(((bf16[8,32,8192]{2,1,0:T(8,128)(2,1)}), bf16[8,32,8192]{2,1,0:T(8,128)(2,1)}, u32[]{:S(2)}, u32[]{:S(2)}) %all-to-all-start.2) | async-done | bytes 4194336 | tf_op jit(solution)/shard_map/all_to_all | solution.py:49
  119.0 5.1 %all-to-all-start.3 = ((bf16[8,32,8192]{2,1,0:T(8,128)(2,1)}), bf16[8,32,8192]{2,1,0:T(8,128)(2,1)}, u32[]{:S(2)}, u32[]{:S(2)}) async-start(bf16[8,32,8192]{2,1,0:T(8,128)(2,1)} %bitcast.111), calls=%async_computation.3 | async-start | bytes 8388608 | tf_op jit(solution)/shard_map/all_to_all | solution.py:49
  124.2 33.2 %fusion.39 = f32[512,8192]{1,0:T(8,128)} fusion(bf16[512,3072]{1,0:T(8,128)(2,1)S(1)} %copy-done.4, bf16[3072,8192]{1,0:T(8,128)(2,1)} %param.22), kind=kOutput, calls=%fused_computation.83 | convolution fusion | flops 25769803776 | bytes 70254592 | tf_op jit(solution)/shard_map/dot_general | solution.py:61
  157.4 18.7 %gather_fusion.5 = bf16[512,8192]{1,0:T(8,128)(2,1)} fusion(bf16[256,8192]{1,0:T(8,128)(2,1)} %bitcast.25, s32[1024]{0:T(1024)S(1)} %pad_clamp_fusion), kind=kCustom, calls=%fused_computation.clone | custom fusion | bytes 16779264 | tf_op jit(solution)/shard_map/jit(_take)/gather | solution.py:52
  176.1 0.0 all-to-all-done.3
  176.1 18.4 %gather_fusion.6 = bf16[512,8192]{1,0:T(8,128)(2,1)} fusion(bf16[256,8192]{1,0:T(8,128)(2,1)} %bitcast.35, s32[1024]{0:T(1024)S(1)} %pad_clamp_fusion), kind=kCustom, calls=%fused_computation.1.clone | custom fusion | bytes 16779264 | tf_op jit(solution)/shard_map/jit(_take)/gather | solution.py:52
  194.5 44.6 %multiply_convert_fusion = bf16[512,8192]{1,0:T(8,128)(2,1)} fusion(bf16[512,8192]{1,0:T(8,128)(2,1)} %fusion, f32[512,8192]{1,0:T(8,128)} %fusion.39, bf16[512,8192]{1,0:T(8,128)(2,1)} %fusion.1, bf16[512,3072]{1,0:T(8,128)(2,1)S(1)} %copy-done.4, bf16[3072,8192]{1,0:T(8,128)(2,1)} %param.23, bf16[512,8192]{1,0:T(8,128)(2,1)} %gather_fusion.6, ...), kind=kOutput, calls=%fused_computation.13 | convolution fusion | flops 25845301248 | bytes 112198656 | tf_op jit(solution)/shard_map/dot_general | solution.py:64
  239.1 0.0 copy-start.15
  239.1 13.5 %gather_fusion.3 = bf16[256,8192]{1,0:T(8,128)(2,1)} fusion(bf16[512,8192]{1,0:T(8,128)(2,1)} %multiply_convert_fusion, s32[1024]{0:T(1024)} %copy-done.13), kind=kCustom, calls=%fused_computation.5 | custom fusion | bytes 8389632 | tf_op jit(solution)/shard_map/jit(_take)/gather | solution.py:69
  252.7 2.8 broadcast_select_fusion
  255.5 0.0 slice-start.3
  255.5 53.3 %all_to_all.60 = bf16[8,32,8192]{2,1,0:T(8,128)(2,1)S(1)} all-to-all(bf16[8,32,8192]{2,1,0:T(8,128)(2,1)S(1)} %broadcast_select_fusion), channel_id=1, replica_groups=mesh['replica'=2,'data'=8] {'data'}, dimensions={0} | all-to-all | bytes 8388608 | tf_op jit(solution)/shard_map/all_to_all | solution.py:49
  308.8 0.0 slice-done.2
  308.8 2.4 fusion.45
  311.2 0.0 copy-done.6
  311.2 0.0 copy-done.8
  311.2 2.2 fusion.8
  313.4 3.9 %all-to-all-start.5 = ((bf16[8,32,3072]{2,1,0:T(8,128)(2,1)}), bf16[8,32,3072]{2,1,0:T(8,128)(2,1)S(1)}, u32[]{:S(2)}, u32[]{:S(2)}) async-start(bf16[8,32,3072]{2,1,0:T(8,128)(2,1)} %bitcast.46), calls=%async_computation.5 | async-start | bytes 3145728 | tf_op jit(solution)/shard_map/all_to_all | solution.py:49
  317.3 0.0 copy-start.18
  317.3 7.1 %fusion.44 = f32[512,256]{0,1:S(1)} fusion(bf16[512,8192]{1,0:T(8,128)(2,1)} %multiply_convert_fusion, bf16[8192,256]{0,1:T(8,128)(2,1)} %bitcast.130), kind=kOutput, calls=%fused_computation.88 | convolution fusion | flops 2147483648 | bytes 13107200
  324.4 2.7 fusion.6
  327.1 11.1 %all-to-all-done.5 = bf16[8,32,3072]{2,1,0:T(8,128)(2,1)S(1)} async-done(((bf16[8,32,3072]{2,1,0:T(8,128)(2,1)}), bf16[8,32,3072]{2,1,0:T(8,128)(2,1)S(1)}, u32[]{:S(2)}, u32[]{:S(2)}) %all-to-all-start.5) | async-done | bytes 1572896 | tf_op jit(solution)/shard_map/all_to_all | solution.py:49
  338.2 3.8 %gather_fusion.4 = bf16[512,3072]{1,0:T(8,128)(2,1)} fusion(bf16[256,3072]{1,0:T(8,128)(2,1)S(1)} %bitcast.109, s32[1024]{0:T(1024)S(1)} %pad_clamp_fusion), kind=kCustom, calls=%fused_computation.6 | custom fusion | bytes 6293504 | tf_op jit(solution)/shard_map/jit(_take)/gather | solution.py:52
  342.0 36.3 %add_convert_fusion = bf16[512,3072]{1,0:T(8,128)(2,1)} fusion(bf16[512,3072]{1,0:T(8,128)(2,1)} %fusion.6, bf16[512,3072]{1,0:T(8,128)(2,1)} %param.20, bf16[512,8192]{1,0:T(8,128)(2,1)} %multiply_convert_fusion, bf16[8192,3072]{1,0:T(8,128)(2,1)} %param.24, bf16[512,3072]{1,0:T(8,128)(2,1)} %gather_fusion.4, pred[512]{0:T(512)(128)(4,1)S(1)} %get-tuple-element.8, ...), kind=kOutput, calls=%fused_computation.22 | convolution fusion | flops 25783959552 | bytes 71304192 | tf_op jit(solution)/shard_map/dot_general | solution.py:71
  (46 shorter events, 0.1 us)
Async XLA Ops:
  0.0 54.8 %copy-start = (bf16[8,3072,64]{1,2,0:T(8,128)(2,1)S(1)}, bf16[8,3072,64]{1,2,0:T(8,128)(2,1)}, u32[]{:S(2)}) copy-start(bf16[8,3072,64]{1,2,0:T(8,128)(2,1)} %param.25) | copy-start | bytes 9437188
  0.0 11.9 %copy-start.2 = (s32[512]{0:T(512)S(1)}, s32[512]{0:T(512)}, u32[]{:S(2)}) copy-start(s32[512]{0:T(512)} %param.21) | copy-start | bytes 6148
  0.9 82.8 %copy-start.11 = (bf16[512,4]{0,1:T(4,128)(2,1)}, bf16[512,4]{0,1:T(4,128)(2,1)S(1)}, u32[]{:S(2)}) copy-start(bf16[512,4]{0,1:T(4,128)(2,1)S(1)} %get-tuple-element.11) | copy-start | bytes 12292
  12.0 14.8 %copy-start.13 = (s32[1024]{0:T(1024)}, s32[1024]{0:T(1024)S(1)}, u32[]{:S(2)}) copy-start(s32[1024]{0:T(1024)S(1)} %pad_clamp_fusion.1) | copy-start | bytes 12292
  14.7 14.9 %all-to-all-start.1 = ((s32[8,32,1]{1,2,0:T(1,128)}), s32[8,32,1]{1,2,0:T(1,128)S(1)}, u32[]{:S(2)}, u32[]{:S(2)}) async-start(s32[8,32,1]{1,2,0:T(1,128)} %bitcast.22), calls=%async_computation.1 | async-start | bytes 8192 | tf_op jit(solution)/shard_map/all_to_all | solution.py:49
  20.2 6.6 %copy-start.14 = (pred[8,32]{1,0:T(8,128)(4,1)}, pred[8,32]{1,0:T(8,128)(4,1)S(1)}, u32[]{:S(2)}) copy-start(pred[8,32]{1,0:T(8,128)(4,1)S(1)} %compare_and_fusion) | copy-start | bytes 772
  29.6 25.2 %all-to-all-start = ((bf16[8,32,3072]{2,1,0:T(8,128)(2,1)}), bf16[8,32,3072]{2,1,0:T(8,128)(2,1)}, u32[]{:S(2)}, u32[]{:S(2)}) async-start(bf16[8,32,3072]{2,1,0:T(8,128)(2,1)} %broadcast_select_fusion.1), calls=%async_computation | async-start | bytes 3145728 | tf_op jit(solution)/shard_map/all_to_all | solution.py:49
  36.6 5.2 %copy-start.3 = (bf16[512,3072]{1,0:T(8,128)(2,1)S(1)}, bf16[512,3072]{1,0:T(8,128)(2,1)}, u32[]{:S(2)}) copy-start(bf16[512,3072]{1,0:T(8,128)(2,1)} %param.20) | copy-start | bytes 9437188
  36.6 5.2 %copy-start.17 = (bf16[4,3072,64]{1,2,0:T(8,128)(2,1)S(1)}, bf16[4,3072,64]{1,2,0:T(8,128)(2,1)}, u32[]{:S(2)}) copy-start(bf16[4,3072,64]{1,2,0:T(8,128)(2,1)} %param.34) | copy-start | bytes 4718596
  43.7 48.1 %copy-start.7 = (bf16[256,8]{0,1:T(8,128)(2,1)}, bf16[256,8]{0,1:T(8,128)(2,1)S(1)}, u32[]{:S(2)}) copy-start(bf16[256,8]{0,1:T(8,128)(2,1)S(1)} %fusion.27) | copy-start | bytes 12292
  65.1 10.7 %copy-start.10 = (f32[512,256]{0,1:S(1)}, f32[512,256]{0,1}, u32[]{:S(2)}) copy-start(f32[512,256]{0,1} %fusion.42) | copy-start | bytes 1572868
  65.1 54.0 %all-to-all-start.2 = ((bf16[8,32,8192]{2,1,0:T(8,128)(2,1)}), bf16[8,32,8192]{2,1,0:T(8,128)(2,1)}, u32[]{:S(2)}, u32[]{:S(2)}) async-start(bf16[8,32,8192]{2,1,0:T(8,128)(2,1)} %bitcast.110), calls=%async_computation.2 | async-start | bytes 8388608 | tf_op jit(solution)/shard_map/all_to_all | solution.py:49
  75.8 8.0 %copy-start.5 = (bf16[4,64,8192]{2,1,0:T(8,128)(2,1)S(1)}, bf16[4,64,8192]{2,1,0:T(8,128)(2,1)}, u32[]{:S(2)}) copy-start(bf16[4,64,8192]{2,1,0:T(8,128)(2,1)} %param.33) | copy-start | bytes 12582916
  75.8 8.0 %copy-start.9 = (f32[512,256]{0,1:S(1)}, f32[512,256]{0,1}, u32[]{:S(2)}) copy-start(f32[512,256]{0,1} %fusion.40) | copy-start | bytes 1572868
  75.8 16.1 %slice-start = ((s8[8388608]{0:T(1024)(128)(4,1)}), s8[4194304]{0:T(1024)(128)(4,1)S(1)}, s32[]{:S(2)}) async-start(s8[8388608]{0:T(1024)(128)(4,1)} %bitcast.113), calls=%async_computation.6 | async-start | bytes 8388608
  83.8 5.7 %copy-start.16 = (bf16[8,3072,64]{1,2,0:T(8,128)(2,1)S(1)}, bf16[8,3072,64]{1,2,0:T(8,128)(2,1)}, u32[]{:S(2)}) copy-start(bf16[8,3072,64]{1,2,0:T(8,128)(2,1)} %param.27) | copy-start | bytes 9437188
  83.8 8.1 %slice-start.1 = ((s8[8388608]{0:T(1024)(128)(4,1)}), s8[4194304]{0:T(1024)(128)(4,1)S(1)}, s32[]{:S(2)}) async-start(s8[8388608]{0:T(1024)(128)(4,1)} %bitcast.113), calls=%async_computation.7 | async-start | bytes 8388608
  119.0 5.1 %copy-start.4 = (bf16[512,3072]{1,0:T(8,128)(2,1)S(1)}, bf16[512,3072]{1,0:T(8,128)(2,1)}, u32[]{:S(2)}) copy-start(bf16[512,3072]{1,0:T(8,128)(2,1)} %param.20) | copy-start | bytes 9437188
  119.0 57.1 %all-to-all-start.3 = ((bf16[8,32,8192]{2,1,0:T(8,128)(2,1)}), bf16[8,32,8192]{2,1,0:T(8,128)(2,1)}, u32[]{:S(2)}, u32[]{:S(2)}) async-start(bf16[8,32,8192]{2,1,0:T(8,128)(2,1)} %bitcast.111), calls=%async_computation.3 | async-start | bytes 8388608 | tf_op jit(solution)/shard_map/all_to_all | solution.py:49
  239.1 13.6 %copy-start.15 = (pred[8,32]{1,0:T(8,128)(4,1)S(1)}, pred[8,32]{1,0:T(8,128)(4,1)}, u32[]{:S(2)}) copy-start(pred[8,32]{1,0:T(8,128)(4,1)} %copy-done.14) | copy-start | bytes 772
  252.7 56.1 %slice-start.2 = ((s8[8388608]{0:T(1024)(128)(4,1)}), s8[4194304]{0:T(1024)(128)(4,1)S(1)}, s32[]{:S(2)}) async-start(s8[8388608]{0:T(1024)(128)(4,1)} %bitcast.127), calls=%async_computation.8 | async-start | bytes 8388608
  255.5 53.3 %slice-start.3 = ((s8[8388608]{0:T(1024)(128)(4,1)}), s8[4194304]{0:T(1024)(128)(4,1)S(1)}, s32[]{:S(2)}) async-start(s8[8388608]{0:T(1024)(128)(4,1)} %bitcast.127), calls=%async_computation.9 | async-start | bytes 8388608
  308.8 2.4 copy-start.6
  308.8 2.4 copy-start.8
  313.4 24.8 %all-to-all-start.5 = ((bf16[8,32,3072]{2,1,0:T(8,128)(2,1)}), bf16[8,32,3072]{2,1,0:T(8,128)(2,1)S(1)}, u32[]{:S(2)}, u32[]{:S(2)}) async-start(bf16[8,32,3072]{2,1,0:T(8,128)(2,1)} %bitcast.46), calls=%async_computation.5 | async-start | bytes 3145728 | tf_op jit(solution)/shard_map/all_to_all | solution.py:49
  317.3 7.1 %copy-start.12 = (bf16[512,4]{0,1:T(4,128)(2,1)S(1)}, bf16[512,4]{0,1:T(4,128)(2,1)}, u32[]{:S(2)}) copy-start(bf16[512,4]{0,1:T(4,128)(2,1)} %copy-done.11) | copy-start | bytes 12292
  317.3 7.1 %copy-start.18 = (bf16[4,64,3072]{2,1,0:T(8,128)(2,1)S(1)}, bf16[4,64,3072]{2,1,0:T(8,128)(2,1)}, u32[]{:S(2)}) copy-start(bf16[4,64,3072]{2,1,0:T(8,128)(2,1)} %param.37) | copy-start | bytes 4718596
  342.0 36.3 %copy-start.1 = (bf16[8,3072,64]{1,2,0:T(8,128)(2,1)S(1)}, bf16[8,3072,64]{1,2,0:T(8,128)(2,1)}, u32[]{:S(2)}) copy-start(bf16[8,3072,64]{1,2,0:T(8,128)(2,1)} %param.25) | copy-start | bytes 9437188
where the time goes:
time: 385 us; the launch traced here: 379 us
  matrix products  166 us (43%)
  local copies, waits for them, and re-layouts  68.8 us (18%)
  blocking collectives  53.3 us (14%)
  waiting for transfers between devices  44.9 us (12%)
  starting transfers between devices  23.7 us (6%)
  other arithmetic  21.8 us (6%)
    all_to_all x1, blocking collectives, exchange(): return lax.all_to_all(send_rows, 'data', 0, 0, tiled=True)  53.3 us
    all_to_all x5, waiting for transfers between devices, exchange(): return lax.all_to_all(send_rows, 'data', 0, 0, tiled=True)  44.9 us
    dot_general x1, matrix products, device_step(): jnp.dot(x, w_up, preferred_element_type=jnp.float32)  44.6 us
    gather x3, local copies, waits for them, and re-layouts, to_tokens(): jnp.take(back_rows, tok_slot, axis=0).astype(jnp.float32)  40.9 us
    dot_general x1, matrix products, device_step(): jnp.dot(hidden, w_down, preferred_element_type=jnp.float32)  36.3 us
    dot_general x1, matrix products, device_step(): jnp.dot(x, w_gate, preferred_element_type=jnp.float32)  33.2 us
    dot_general x6, matrix products, adapter_delta(): jnp.einsum('mnr,nrf->mf', low_rank, b_set, preferred_element_type=jnp.flo...  30.7 us
    all_to_all x5, starting transfers between devices, exchange(): return lax.all_to_all(send_rows, 'data', 0, 0, tiled=True)  23.7 us
  transfers between devices with their start and end apart: 5, of which 3 were waited for; matrix products, arithmetic and copies ran while one was open for 28% of the time, Pallas kernels for 0%

commit v1 on v0

v1 whole, which is shorter than its diff:
```python
import functools

import jax
import jax.numpy as jnp
from jax import lax
from jax.experimental import pallas as pl
from jax.experimental.pallas import tpu as pltpu
from jax.sharding import PartitionSpec as P

LORA_ALPHA = 32
MESH = pl.DeviceIdType.MESH
F32 = jnp.float32
BF16 = jnp.bfloat16

TN = 512
FIRST = 8


def dot(a, b):
    return jnp.dot(a, b, preferred_element_type=F32)


def dot_t(a, b):
    return lax.dot_general(a, b, (((1,), (1,)), ((), ())), preferred_element_type=F32)


def positions(ids, hot_ids, n_hot, group, n_local, cap):
    tokens = ids.shape[1]
    kept = tokens - group * cap
    is_hot = ids < 0
    hot_idx = jnp.zeros_like(ids)
    for j in range(n_hot):
        match = ids == hot_ids[j]
        is_hot = is_hot | match
        hot_idx = jnp.where(match, j, hot_idx)
    owner = jnp.where(is_hot, group, ids // n_local)
    local = ids - (ids // n_local) * n_local
    cls = jnp.where(is_hot, n_local + hot_idx, local)
    rows = 2 * group
    kind = lax.broadcasted_iota(jnp.int32, (rows, tokens), 0)
    member = (kind == jnp.broadcast_to(owner, (rows, tokens))).astype(F32)
    before = lax.broadcasted_iota(jnp.int32, (tokens, tokens), 0) < lax.broadcasted_iota(jnp.int32, (tokens, tokens), 1)
    cum = dot(member.astype(BF16), before.astype(BF16))
    rank = jnp.sum(member * cum, axis=0, keepdims=True)
    counts = jnp.sum(member, axis=1, keepdims=True)
    sub = lax.broadcasted_iota(jnp.int32, (rows, 1), 0)
    holes = jnp.where(sub < group, cap - counts, 0.0)
    lower = lax.broadcasted_iota(jnp.int32, (rows, rows), 1) < lax.broadcasted_iota(jnp.int32, (rows, rows), 0)
    hole_start = dot(lower.astype(BF16), jnp.broadcast_to(holes, (rows, 128)).astype(BF16))[:, 0:1]
    spill = jnp.broadcast_to(rank - kept, (rows, tokens))
    takes = (spill >= hole_start) & (spill < hole_start + holes)
    base = kept + cap * sub.astype(F32) + counts - hole_start
    filled = jnp.sum(jnp.where(takes, base + spill, 0.0), axis=0, keepdims=True)
    own = kept + cap * owner.astype(F32) + rank
    pos = jnp.where(is_hot, jnp.where(rank < kept, rank, filled), own)
    return pos, cls.astype(F32)


def masked(low, cls, first_group, rank):
    per = 128 // rank
    lane = lax.broadcasted_iota(jnp.int32, (low.shape[0], 128), 1) // rank
    parts = []
    for k in range(low.shape[1] // 128):
        here = (lane + per * (first_group + k)).astype(F32) == cls
        parts.append(jnp.where(here, low[:, k * 128:(k + 1) * 128], 0.0).astype(BF16))
    return jnp.concatenate(parts, axis=1)


def mlp_kernel(group, n_local, n_hot, rank, scale,
               hot_ids, ids, x_hbm, wg_hbm, wu_hbm, wd_hbm,
               ag_hbm, bg_hbm, au_hbm, bu_hbm, ad_hbm, bd_hbm,
               hag_hbm, hbg_hbm, hau_hbm, hbu_hbm, had_hbm, hbd_hbm,
               out_hbm,
               x_v, xsend, xa, h, pg, pu, pd, pdm, at, wbuf, bbuf, adbuf, y_send, y_back, y_kept, o_stage, unperm,
               x_sem, at_sem, w_sem, o_sem, s1, r1, s2, r2):
    me = lax.axis_index("data")
    tokens, d_model = x_hbm.shape
    d_ff = wg_hbm.shape[1]
    cap = tokens // (2 * group)
    half = group * cap
    n_own = n_local * rank
    n_hr = n_hot * rank
    n_all = n_own + n_hr
    n_tiles = d_ff // TN
    d_tiles = d_model // TN
    k_half = d_ff // 2
    kept = pl.ds(0, half)
    recv = pl.ds(half, half)
    hot_cols = pl.ds(n_own, n_hr)
    hot_group = n_own // 128

    def cp(src, dst, sem):
        return pltpu.make_async_copy(src, dst, sem)

    def gu_copies(tile, slot, full):
        cols = pl.ds(pl.multiple_of(tile * TN, TN), TN)
        out = [
            cp(wg_hbm.at[:, cols], wbuf.at[slot, 0, pl.ds(0, d_model)], w_sem.at[slot, 0]),
            cp(wu_hbm.at[:, cols], wbuf.at[slot, 1, pl.ds(0, d_model)], w_sem.at[slot, 1]),
            cp(hbg_hbm.at[:, cols], bbuf.at[slot, 0, hot_cols], w_sem.at[slot, 2]),
            cp(hbu_hbm.at[:, cols], bbuf.at[slot, 1, hot_cols], w_sem.at[slot, 3]),
        ]
        if full:
            out += [
                cp(bg_hbm.at[:, cols], bbuf.at[slot, 0, pl.ds(0, n_own)], w_sem.at[slot, 4]),
                cp(bu_hbm.at[:, cols], bbuf.at[slot, 1, pl.ds(0, n_own)], w_sem.at[slot, 5]),
                cp(ad_hbm.at[:, cols], adbuf.at[slot, pl.ds(0, n_own)], w_sem.at[slot, 6]),
                cp(had_hbm.at[:, cols], adbuf.at[slot, hot_cols], w_sem.at[slot, 7]),
            ]
        return out

    def down_copies(tile, slot):
        cols = pl.ds(pl.multiple_of(tile * TN, TN), TN)
        return [
            cp(wd_hbm.at[pl.ds(0, k_half), cols], wbuf.at[slot, 0], w_sem.at[slot, 0]),
            cp(wd_hbm.at[pl.ds(k_half, k_half), cols], wbuf.at[slot, 1], w_sem.at[slot, 1]),
            cp(bd_hbm.at[:, cols], bbuf.at[slot, 0, pl.ds(0, n_own)], w_sem.at[slot, 4]),
            cp(hbd_hbm.at[:, cols], bbuf.at[slot, 0, hot_cols], w_sem.at[slot, 2]),
        ]

    def start(copies):
        for c in copies:
            c.start()

    def wait(copies):
        for c in copies:
            c.wait()

    x_copy = cp(x_hbm, x_v, x_sem)
    x_copy.start()
    at_hot = [cp(hag_hbm, at.at[0, hot_cols], at_sem.at[0]), cp(hau_hbm, at.at[1, hot_cols], at_sem.at[1])]
    at_own = [cp(ag_hbm, at.at[0, pl.ds(0, n_own)], at_sem.at[2]), cp(au_hbm, at.at[1, pl.ds(0, n_own)], at_sem.at[3])]
    start(at_hot)
    start(gu_copies(0, 0, False))
    start(at_own)

    barrier = pltpu.get_barrier_semaphore()
    for d in range(1, group):
        pl.semaphore_signal(barrier, inc=1, device_id={"data": lax.rem(me + d, group)}, device_id_type=MESH)

    pos, cls = positions(ids[...], hot_ids, n_hot, group, n_local, cap)
    place = jnp.broadcast_to(pos.astype(jnp.int32), (tokens, tokens))
    perm = (place == lax.broadcasted_iota(jnp.int32, (tokens, tokens), 0)).astype(BF16)
    cls_rows = dot_t(perm, jnp.broadcast_to(cls, (128, tokens)).astype(BF16)).astype(BF16)
    pos_col = jnp.transpose(jnp.broadcast_to(pos, (128, tokens)))[:, 0:1].astype(jnp.int32)
    unperm[...] = (pos_col == lax.broadcasted_iota(jnp.int32, (tokens, tokens), 1)).astype(BF16)
    xsend[:, pl.ds(d_model, 128)] = cls_rows[half:]
    xa[kept, pl.ds(d_model, 128)] = cls_rows[:half]
    x_copy.wait()
    for n in range(d_tiles):
        cols = pl.ds(n * TN, TN)
        moved = dot(perm, x_v[:, cols])
        xsend[:, cols] = moved[half:].astype(BF16)
        xa[kept, cols] = moved[:half].astype(BF16)

    pl.semaphore_wait(barrier, group - 1)
    my_block = pl.ds(pl.multiple_of(me * cap, cap), cap)
    my_rows = pl.ds(pl.multiple_of(half + me * cap, cap), cap)

    def x_remote(d):
        to = lax.rem(me + d, group)
        return pltpu.make_async_remote_copy(
            src_ref=xsend.at[pl.ds(pl.multiple_of(to * cap, cap), cap)], dst_ref=xa.at[my_rows],
            send_sem=s1.at[d], recv_sem=r1.at[d], device_id={"data": to}, device_id_type=MESH)

    for d in range(1, group):
        x_remote(d).start()
    xa[my_rows, :] = xsend[my_block, :]

    def lora(low, b):
        return (scale * dot(low, b)).astype(BF16).astype(F32)

    def act(g, u):
        return (g * jax.nn.sigmoid(g) * u).astype(BF16)

    cls_kept = xa[kept, pl.ds(d_model, 128)].astype(F32)
    for i, p in ((0, pg), (1, pu)):
        at_hot[i].wait()
        low = dot_t(xa[kept, pl.ds(0, d_model)], at[i, hot_cols, :])
        p[kept, hot_cols] = masked(low.astype(BF16).astype(F32), cls_kept, hot_group, rank)

    def first_step(s, carry):
        slot = lax.rem(s, 2)

        @pl.when(s + 1 < FIRST)
        def _():
            start(gu_copies(s + 1, 1 - slot, False))

        @pl.when(s + 1 == FIRST)
        def _():
            start(gu_copies(0, 1 - slot, True))

        wait(gu_copies(s, slot, False))
        xk = xa[kept, pl.ds(0, d_model)]
        g = dot(xk, wbuf[slot, 0, pl.ds(0, d_model), :]) + lora(pg[kept, hot_cols], bbuf[slot, 0, hot_cols, :])
        u = dot(xk, wbuf[slot, 1, pl.ds(0, d_model), :]) + lora(pu[kept, hot_cols], bbuf[slot, 1, hot_cols, :])
        h[kept, pl.ds(pl.multiple_of(s * TN, TN), TN)] = act(g, u)
        return carry

    lax.fori_loop(0, FIRST, first_step, 0)

    for d in range(1, group):
        x_remote(d).wait_recv()
    cls_recv = xa[recv, pl.ds(d_model, 128)].astype(F32)
    for i, p in ((0, pg), (1, pu)):
        at_own[i].wait()
        low = dot_t(xa[recv, pl.ds(0, d_model)], at[i])
        p[recv, :] = masked(low.astype(BF16).astype(F32), cls_recv, 0, rank)
    pd[...] = jnp.zeros_like(pd)

    def add_low(slot, cols):
        pd[kept, hot_cols] += dot_t(h[kept, cols], adbuf[slot, hot_cols, :])
        pd[recv, :] += dot_t(h[recv, cols], adbuf[slot])

    def second_step(s, carry):
        slot = lax.rem(s + FIRST, 2)
        start(gu_copies(s + 1, 1 - slot, True))
        wait(gu_copies(s, slot, True))
        cols = pl.ds(pl.multiple_of(s * TN, TN), TN)
        xr = xa[recv, pl.ds(0, d_model)]
        g = dot(xr, wbuf[slot, 0, pl.ds(0, d_model), :]) + lora(pg[recv, :], bbuf[slot, 0])
        u = dot(xr, wbuf[slot, 1, pl.ds(0, d_model), :]) + lora(pu[recv, :], bbuf[slot, 1])
        h[recv, cols] = act(g, u)
        add_low(slot, cols)
        return carry

    lax.fori_loop(0, FIRST, second_step, 0)

    def both_lora(p, slot, i, n_rows=None):
        return lora(p[kept, hot_cols], bbuf[slot, i, hot_cols, :]), lora(p[recv, :], bbuf[slot, i])

    def third_step(s, carry):
        slot = lax.rem(s + FIRST, 2)

        @pl.when(s + 1 < n_tiles)
        def _():
            start(gu_copies(s + 1, 1 - slot, True))

        @pl.when(s + 1 == n_tiles)
        def _():
            start(down_copies(0, 1 - slot))

        wait(gu_copies(s, slot, True))
        cols = pl.ds(pl.multiple_of(s * TN, TN), TN)
        xx = xa[:, pl.ds(0, d_model)]
        g = dot(xx, wbuf[slot, 0, pl.ds(0, d_model), :])
        u = dot(xx, wbuf[slot, 1, pl.ds(0, d_model), :])
        gk, gr = both_lora(pg, slot, 0)
        uk, ur = both_lora(pu, slot, 1)
        h[kept, cols] = act(g[:half] + gk, u[:half] + uk)
        h[recv, cols] = act(g[half:] + gr, u[half:] + ur)
        add_low(slot, cols)
        return carry

    lax.fori_loop(FIRST, n_tiles, third_step, 0)
    slot0 = (n_tiles + FIRST) % 2

    pdm[kept, hot_cols] = masked(pd[kept, hot_cols].astype(BF16).astype(F32), cls_kept, hot_group, rank)
    pdm[recv, :] = masked(pd[recv, :].astype(BF16).astype(F32), cls_recv, 0, rank)

    def y_remote(n, d):
        to = lax.rem(me + d, group)
        return pltpu.make_async_remote_copy(
            src_ref=y_send.at[n, pl.ds(pl.multiple_of(to * cap, cap), cap)], dst_ref=y_back.at[n, my_block],
            send_sem=s2.at[n, d], recv_sem=r2.at[n, d], device_id={"data": to}, device_id_type=MESH)

    def rows_out(n, slot, rows, low):
        cols = pl.ds(pl.multiple_of(n * TN, TN), TN)
        y = dot(h[rows, pl.ds(0, k_half)], wbuf[slot, 0]) + dot(h[rows, pl.ds(k_half, k_half)], wbuf[slot, 1])
        return (xa[rows, cols].astype(F32) + (y + low)).astype(BF16)

    def down_recv(n, slot):
        y_send[n] = rows_out(n, slot, recv, lora(pdm[recv, :], bbuf[slot, 0]))

    def down_kept(n, slot):
        y_kept[n] = rows_out(n, slot, kept, lora(pdm[kept, hot_cols], bbuf[slot, 0, hot_cols, :]))

    def send_back(n):
        for d in range(1, group):
            y_remote(n, d).start()
        y_back[n, my_block, :] = y_send[n, my_block, :]

    def out_copy(n, slot):
        return cp(o_stage.at[slot], out_hbm.at[:, pl.ds(pl.multiple_of(n * TN, TN), TN)], o_sem.at[slot])

    def finish(n, slot):
        for d in range(1, group):
            y_remote(n, d).wait_recv()
        o_stage[slot] = (dot(unperm[:, pl.ds(0, half)], y_kept[n]) + dot(unperm[:, pl.ds(half, half)], y_back[n])).astype(BF16)
        out_copy(n, slot).start()

    def down_step(n, carry):
        slot = lax.rem(n + slot0, 2)

        @pl.when(n + 1 < d_tiles)
        def _():
            start(down_copies(n + 1, 1 - slot))

        wait(down_copies(n, slot))
        down_recv(n, slot)
        send_back(n)
        down_kept(n, slot)

        @pl.when(n > 0)
        def _():
            @pl.when(n > 2)
            def _():
                out_copy(n - 3, lax.rem(n + 1, 2)).wait()
            finish(n - 1, lax.rem(n + 1, 2))
        return carry

    lax.fori_loop(0, d_tiles, down_step, 0)
    last = d_tiles - 1
    out_copy(last - 2, last % 2).wait()
    finish(last, last % 2)
    out_copy(last - 1, 1 - last % 2).wait()
    out_copy(last, last % 2).wait()

    for d in range(1, group):
        x_remote(d).wait_send()

    def drain(n, carry):
        for d in range(1, group):
            y_remote(n, d).wait_send()
        return carry

    lax.fori_loop(0, d_tiles, drain, 0)


def solution(mesh):
    group = mesh.shape["data"]
    token_spec = P(("replica", "data"), None)
    store_spec = P("data", None, None)
    full_mat = P(None, None)
    full_set = P(None, None, None)
    in_specs = (token_spec, P(("replica", "data")), full_mat, full_mat, full_mat) + (store_spec,) * 6 + (P(None),) + (full_set,) * 6

    def device_step(x, adapter_id, w_gate, w_up, w_down, a_gate, b_gate, a_up, b_up, a_down, b_down, hot_ids, hot_a_gate, hot_b_gate, hot_a_up, hot_b_up, hot_a_down, hot_b_down):
        tokens, d_model = x.shape
        d_ff = w_gate.shape[1]
        n_local, _, rank = a_gate.shape
        n_hot = hot_ids.shape[0]
        cap = tokens // (2 * group)
        half = group * cap
        n_all = (n_local + n_hot) * rank
        d_tiles = d_model // TN

        def a_t(a):
            return jnp.swapaxes(a, 1, 2).reshape(a.shape[0] * rank, a.shape[1])

        def b_flat(b):
            return b.reshape(b.shape[0] * rank, b.shape[2])

        hbm = pl.BlockSpec(memory_space=pl.ANY)
        kernel = functools.partial(mlp_kernel, group, n_local, n_hot, rank, LORA_ALPHA / rank)
        return pl.pallas_call(
            kernel,
            out_shape=jax.ShapeDtypeStruct(x.shape, x.dtype),
            in_specs=[pl.BlockSpec(memory_space=pltpu.SMEM), pl.BlockSpec(memory_space=pltpu.VMEM)] + [hbm] * 16,
            out_specs=hbm,
            scratch_shapes=[
                pltpu.VMEM((tokens, d_model), BF16),
                pltpu.VMEM((half, d_model + 128), BF16),
                pltpu.VMEM((tokens, d_model + 128), BF16),
                pltpu.VMEM((tokens, d_ff), BF16),
                pltpu.VMEM((tokens, n_all), BF16),
                pltpu.VMEM((tokens, n_all), BF16),
                pltpu.VMEM((tokens, n_all), F32),
                pltpu.VMEM((tokens, n_all), BF16),
                pltpu.VMEM((2, n_all, d_model), BF16),
                pltpu.VMEM((2, 2, d_ff // 2, TN), BF16),
                pltpu.VMEM((2, 2, n_all, TN), BF16),
                pltpu.VMEM((2, n_all, TN), BF16),
                pltpu.VMEM((d_tiles, half, TN), BF16),
                pltpu.VMEM((d_tiles, half, TN), BF16),
                pltpu.VMEM((d_tiles, half, TN), BF16),
                pltpu.VMEM((2, tokens, TN), BF16),
                pltpu.VMEM((tokens, tokens), BF16),
                pltpu.SemaphoreType.DMA,
                pltpu.SemaphoreType.DMA((4,)),
                pltpu.SemaphoreType.DMA((2, 8)),
                pltpu.SemaphoreType.DMA((2,)),
                pltpu.SemaphoreType.DMA((group,)),
                pltpu.SemaphoreType.DMA((group,)),
                pltpu.SemaphoreType.DMA((d_tiles, group)),
                pltpu.SemaphoreType.DMA((d_tiles, group)),
            ],
            compiler_params=pltpu.CompilerParams(
                collective_id=0, has_side_effects=True, vmem_limit_bytes=67043328),
        )(hot_ids, adapter_id.reshape(1, tokens), x, w_gate, w_up, w_down,
          a_t(a_gate), b_flat(b_gate), a_t(a_up), b_flat(b_up), a_t(a_down), b_flat(b_down),
          a_t(hot_a_gate), b_flat(hot_b_gate), a_t(hot_a_up), b_flat(hot_b_up), a_t(hot_a_down), b_flat(hot_b_down))

    return jax.shard_map(device_step, mesh=mesh, in_specs=in_specs, out_specs=token_spec, check_vma=False)
```

time: 385 us -> 136 us (0.35); the launches traced: 379 us -> 136 us
  matrix products: 166 us -> 0 us
  Pallas kernels: 0 us -> 132 us
  local copies, waits for them, and re-layouts: 68.8 us -> 3.76 us
  blocking collectives: 53.3 us -> 0 us
  waiting for transfers between devices: 44.9 us -> 0 us
  starting transfers between devices: 23.7 us -> 0 us
  other arithmetic: 21.8 us -> 0 us
    dot_general x9 -> x0, matrix products: 145 us -> none  [the longest x1 44.6 us: device_step(): jnp.dot(x, w_up, preferred_element_type=jnp.float32)]
    pallas_call x0 -> x1, Pallas kernels: none -> 132 us  [device_step(): pl.pallas_call(kernel, out_shape=jax.ShapeDtypeStruct(x.shape, x.dtype),...]
    gather x11 -> x0, local copies, waits for them, and re-layouts: 65.8 us -> none  [the longest x3 40.9 us: to_tokens(): jnp.take(back_rows, tok_slot, axis=0).astype(jnp.float32)]
    all_to_all x1 -> x0, blocking collectives: 53.3 us -> none  [exchange(): return lax.all_to_all(send_rows, 'data', 0, 0, tiled=True)]
    all_to_all x5 -> x0, waiting for transfers between devices: 44.9 us -> none  [exchange(): return lax.all_to_all(send_rows, 'data', 0, 0, tiled=True)]
    all_to_all x5 -> x0, starting transfers between devices: 23.7 us -> none  [exchange(): return lax.all_to_all(send_rows, 'data', 0, 0, tiled=True)]
    unnamed x6 -> x0, matrix products: 20.7 us -> none
    select_n x7 -> x0, other arithmetic: 7.04 us -> none  [the longest x1 2.8 us: device_step(): recv_h = exchange(jnp.take(hidden, slot_tok, axis=0))]
  transfers between devices with their start and end apart: 5 -> 0, of which waited for: 3 -> 0; matrix products, arithmetic and copies ran while one was open for 28% -> 0% of each run, Pallas kernels for 0% -> 0%
where the time goes in v1:
time: 136 us
  Pallas kernels  132 us (97%)
  local copies, waits for them, and re-layouts  3.76 us (3%)
    pallas_call x1, Pallas kernels, device_step(): pl.pallas_call(kernel, out_shape=jax.ShapeDtypeStruct(x.shape, x.dtype),...  132 us
    unnamed x1, local copies, waits for them, and re-layouts  3.76 us

profile of v1, /device:TPU:0, one launch (start us, length us, event | category | flops | bytes accessed | tf_op | source)
XLA Modules:
  0.0 135.6 jit_solution(3621800946379774418)
XLA Ops:
  0.0 131.8 %shard_map.172 = bf16[512,3072]{1,0:T(8,128)(2,1)} custom-call(s32[4]{0:T(128)} %hot_ids.1, s32[1,512]{1,0:T(1,128)} %bitcast.37, bf16[512,3072]{1,0:T(8,128)(2,1)} %x_hbm.1, bf16[3072,8192]{1,0:T(8,128)(2,1)} %wg_hbm.1, bf16[3072,8192]{1,0:T(8,128)(2,1)} %wu_hbm.1, bf16[8192,3072]{1,0:T(8,128)(2,1)} %wd_hbm.1, bf16[512,3072]{1,0:T(8,128)(2,1)} %bitcast.31, ...), custom_call_target="tpu_custom_call" | custom-call | tf_op jit(solution)/shard_map/pallas_call | solution.py:356
  131.8 3.8 %copy.20 = bf16[512,3072]{1,0:T(8,128)(2,1)} copy(bf16[512,3072]{1,0:T(8,128)(2,1)} %shard_map.172) | data formatting | bytes 6291456

commit v2 on v1

v2 whole, which is shorter than its diff:
```python
import functools

import jax
import jax.numpy as jnp
from jax import lax
from jax.experimental import pallas as pl
from jax.experimental.pallas import tpu as pltpu
from jax.sharding import PartitionSpec as P

LORA_ALPHA = 32
MESH = pl.DeviceIdType.MESH
F32 = jnp.float32
BF16 = jnp.bfloat16

TN = 512
FIRST = 8


def dot(a, b):
    return jnp.dot(a, b, preferred_element_type=F32)


def dot_t(a, b):
    return lax.dot_general(a, b, (((1,), (1,)), ((), ())), preferred_element_type=F32)


def positions(ids, hot_ids, n_hot, group, n_local, cap):
    tokens = ids.shape[1]
    kept = tokens - group * cap
    is_hot = ids < 0
    hot_idx = jnp.zeros_like(ids)
    for j in range(n_hot):
        match = ids == hot_ids[j]
        is_hot = is_hot | match
        hot_idx = jnp.where(match, j, hot_idx)
    owner = jnp.where(is_hot, group, ids // n_local)
    local = ids - (ids // n_local) * n_local
    cls = jnp.where(is_hot, n_local + hot_idx, local)
    rows = 2 * group
    kind = lax.broadcasted_iota(jnp.int32, (rows, tokens), 0)
    member = (kind == jnp.broadcast_to(owner, (rows, tokens))).astype(F32)
    before = lax.broadcasted_iota(jnp.int32, (tokens, tokens), 0) < lax.broadcasted_iota(jnp.int32, (tokens, tokens), 1)
    cum = dot(member.astype(BF16), before.astype(BF16))
    rank = jnp.sum(member * cum, axis=0, keepdims=True)
    counts = jnp.sum(member, axis=1, keepdims=True)
    sub = lax.broadcasted_iota(jnp.int32, (rows, 1), 0)
    holes = jnp.where(sub < group, cap - counts, 0.0)
    lower = lax.broadcasted_iota(jnp.int32, (rows, rows), 1) < lax.broadcasted_iota(jnp.int32, (rows, rows), 0)
    hole_start = dot(lower.astype(BF16), jnp.broadcast_to(holes, (rows, 128)).astype(BF16))[:, 0:1]
    spill = jnp.broadcast_to(rank - kept, (rows, tokens))
    takes = (spill >= hole_start) & (spill < hole_start + holes)
    base = kept + cap * sub.astype(F32) + counts - hole_start
    filled = jnp.sum(jnp.where(takes, base + spill, 0.0), axis=0, keepdims=True)
    own = kept + cap * owner.astype(F32) + rank
    pos = jnp.where(is_hot, jnp.where(rank < kept, rank, filled), own)
    return pos, cls.astype(F32)


def masked(low, cls, first_group, rank):
    per = 128 // rank
    lane = lax.broadcasted_iota(jnp.int32, (low.shape[0], 128), 1) // rank
    parts = []
    for k in range(low.shape[1] // 128):
        here = (lane + per * (first_group + k)).astype(F32) == cls
        parts.append(jnp.where(here, low[:, k * 128:(k + 1) * 128], 0.0).astype(BF16))
    return jnp.concatenate(parts, axis=1)


def mlp_kernel(group, n_local, n_hot, rank, scale,
               hot_hbm, ids_hbm, x_hbm, wg_hbm, wu_hbm, wd_hbm,
               ag_hbm, bg_hbm, au_hbm, bu_hbm, ad_hbm, bd_hbm,
               hag_hbm, hbg_hbm, hau_hbm, hbu_hbm, had_hbm, hbd_hbm,
               out_hbm,
               hot_ids, ids, xy, xsend, xa, h, pg, pu, pd, pdm, at, wbuf, bbuf, adbuf, y_kept, o_stage, unperm,
               id_sem, x_sem, at_sem, w_sem, d_sem, o_sem, s1, r1, s2, r2):
    me = lax.axis_index("data")
    tokens, d_model = x_hbm.shape
    d_ff = wg_hbm.shape[1]
    cap = tokens // (2 * group)
    half = group * cap
    n_own = n_local * rank
    n_hr = n_hot * rank
    n_tiles = d_ff // TN
    d_tiles = d_model // TN
    kept = pl.ds(0, half)
    recv = pl.ds(half, half)
    own_cols = pl.ds(0, n_own)
    hot_cols = pl.ds(n_own, n_hr)
    hot_group = n_own // 128
    steps = FIRST + n_tiles
    lead = steps % 3
    k_parts = [(k, min(d_model, d_ff - k)) for k in range(0, d_ff, d_model)]
    assert len(k_parts) == 3

    def cp(src, dst, sem):
        return pltpu.make_async_copy(src, dst, sem)

    def tile_cols(tile):
        return pl.ds(tile * TN if isinstance(tile, int) else pl.multiple_of(tile * TN, TN), TN)

    def gu_copies(tile, slot, full):
        cols = tile_cols(tile)
        out = [
            cp(wg_hbm.at[:, cols], wbuf.at[2 * slot], w_sem.at[slot, 0]),
            cp(wu_hbm.at[:, cols], wbuf.at[2 * slot + 1], w_sem.at[slot, 1]),
            cp(hbg_hbm.at[:, cols], bbuf.at[slot, 0, hot_cols], w_sem.at[slot, 2]),
            cp(hbu_hbm.at[:, cols], bbuf.at[slot, 1, hot_cols], w_sem.at[slot, 3]),
        ]
        if full:
            out += [
                cp(bg_hbm.at[:, cols], bbuf.at[slot, 0, own_cols], w_sem.at[slot, 4]),
                cp(bu_hbm.at[:, cols], bbuf.at[slot, 1, own_cols], w_sem.at[slot, 5]),
                cp(ad_hbm.at[:, cols], adbuf.at[slot, own_cols], w_sem.at[slot, 6]),
                cp(had_hbm.at[:, cols], adbuf.at[slot, hot_cols], w_sem.at[slot, 7]),
            ]
        return out

    def down_half(n, i):
        return lax.rem(2 * lead + 3 * lax.rem(n, 2) + i, 6)

    def down_b(n):
        return lax.rem(lead + lax.rem(n, 2), 3)

    def down_copies(n, pieces=(0, 1, 2, 3, 4)):
        cols = tile_cols(n)
        side = lax.rem(n, 2)
        out = []
        for i in pieces:
            if i < 3:
                k, size = k_parts[i]
                src, dst = wd_hbm.at[pl.ds(k, size), cols], wbuf.at[down_half(n, i), pl.ds(0, size)]
            elif i == 3:
                src, dst = bd_hbm.at[:, cols], bbuf.at[down_b(n), 0, own_cols]
            else:
                src, dst = hbd_hbm.at[:, cols], bbuf.at[down_b(n), 0, hot_cols]
            out.append(cp(src, dst, d_sem.at[side, i]))
        return out

    def start(copies):
        for c in copies:
            c.start()

    def wait(copies):
        for c in copies:
            c.wait()

    id_copies = [cp(ids_hbm, ids, id_sem.at[0]), cp(hot_hbm, hot_ids, id_sem.at[1])]
    x_copies = [cp(x_hbm.at[:, pl.ds(n * TN, TN)], xy.at[n], x_sem.at[n]) for n in range(d_tiles)]
    at_hot = [cp(hag_hbm, at.at[0, hot_cols], at_sem.at[0]), cp(hau_hbm, at.at[1, hot_cols], at_sem.at[1])]
    at_own = [cp(ag_hbm, at.at[0, own_cols], at_sem.at[2]), cp(au_hbm, at.at[1, own_cols], at_sem.at[3])]
    start(id_copies)
    start(x_copies)
    start(at_hot)
    start(gu_copies(0, 0, False))
    start(gu_copies(1, 1, False))

    barrier = pltpu.get_barrier_semaphore()
    for d in range(1, group):
        pl.semaphore_signal(barrier, inc=1, device_id={"data": lax.rem(me + d, group)}, device_id_type=MESH)

    wait(id_copies)
    pos, cls = positions(ids[...], hot_ids, n_hot, group, n_local, cap)
    place = jnp.broadcast_to(pos.astype(jnp.int32), (tokens, tokens))
    perm = (place == lax.broadcasted_iota(jnp.int32, (tokens, tokens), 0)).astype(BF16)
    cls_rows = dot_t(perm, jnp.broadcast_to(cls, (128, tokens)).astype(BF16)).astype(BF16)
    xsend[:, pl.ds(d_model, 128)] = cls_rows[half:]
    xa[kept, pl.ds(d_model, 128)] = cls_rows[:half]
    for n in range(d_tiles):
        cols = pl.ds(n * TN, TN)
        x_copies[n].wait()
        moved = dot(perm, xy[n])
        xsend[:, cols] = moved[half:].astype(BF16)
        xa[kept, cols] = moved[:half].astype(BF16)

    pl.semaphore_wait(barrier, group - 1)
    my_block = pl.ds(pl.multiple_of(me * cap, cap), cap)
    my_rows = pl.ds(pl.multiple_of(half + me * cap, cap), cap)

    def x_remote(d):
        to = lax.rem(me + d, group)
        return pltpu.make_async_remote_copy(
            src_ref=xsend.at[pl.ds(pl.multiple_of(to * cap, cap), cap)], dst_ref=xa.at[my_rows],
            send_sem=s1.at[d], recv_sem=r1.at[d], device_id={"data": to}, device_id_type=MESH)

    for d in range(1, group):
        x_remote(d).start()
    xa[my_rows, :] = xsend[my_block, :]
    pos_col = jnp.transpose(jnp.broadcast_to(pos, (128, tokens)))[:, 0:1].astype(jnp.int32)
    unperm[...] = (pos_col == lax.broadcasted_iota(jnp.int32, (tokens, tokens), 1)).astype(BF16)

    def lora(low, b):
        return (scale * dot(low, b)).astype(BF16).astype(F32)

    def act(g, u):
        return (g * jax.nn.sigmoid(g) * u).astype(BF16)

    cls_kept = xa[kept, pl.ds(d_model, 128)].astype(F32)
    for i, p in ((0, pg), (1, pu)):
        at_hot[i].wait()
        low = dot_t(xa[kept, pl.ds(0, d_model)], at[i, hot_cols, :])
        p[kept, hot_cols] = masked(low.astype(BF16).astype(F32), cls_kept, hot_group, rank)

    def first_step(s, carry):
        slot = lax.rem(s, 3)
        ahead = lax.rem(s + 2, 3)
        wait(gu_copies(s, slot, False))

        @pl.when(s + 2 < FIRST)
        def _():
            start(gu_copies(s + 2, ahead, False))

        @pl.when(s + 2 >= FIRST)
        def _():
            start(gu_copies(s + 2 - FIRST, ahead, True))

        @pl.when(s == 0)
        def _():
            start(at_own)

        xk = xa[kept, pl.ds(0, d_model)]
        g = dot(xk, wbuf[2 * slot]) + lora(pg[kept, hot_cols], bbuf[slot, 0, hot_cols, :])
        u = dot(xk, wbuf[2 * slot + 1]) + lora(pu[kept, hot_cols], bbuf[slot, 1, hot_cols, :])
        h[kept, tile_cols(s)] = act(g, u)
        return carry

    lax.fori_loop(0, FIRST, first_step, 0)

    for d in range(1, group):
        x_remote(d).wait_recv()
    cls_recv = xa[recv, pl.ds(d_model, 128)].astype(F32)
    for i, p in ((0, pg), (1, pu)):
        at_own[i].wait()
        low = dot_t(xa[recv, pl.ds(0, d_model)], at[i])
        p[recv, :] = masked(low.astype(BF16).astype(F32), cls_recv, 0, rank)
    pd[...] = jnp.zeros_like(pd)

    def add_low(slot, cols):
        pd[kept, hot_cols] += dot_t(h[kept, cols], adbuf[slot, hot_cols, :])
        pd[recv, :] += dot_t(h[recv, cols], adbuf[slot])

    def second_step(s, carry):
        slot = lax.rem(s + FIRST, 3)
        wait(gu_copies(s, slot, True))
        start(gu_copies(s + 2, lax.rem(s + FIRST + 2, 3), True))
        cols = tile_cols(s)
        xr = xa[recv, pl.ds(0, d_model)]
        g = dot(xr, wbuf[2 * slot]) + lora(pg[recv, :], bbuf[slot, 0])
        u = dot(xr, wbuf[2 * slot + 1]) + lora(pu[recv, :], bbuf[slot, 1])
        h[recv, cols] = act(g, u)
        add_low(slot, cols)
        return carry

    lax.fori_loop(0, FIRST, second_step, 0)

    def third_step(s, carry):
        slot = lax.rem(s + FIRST, 3)
        wait(gu_copies(s, slot, True))

        @pl.when(s + 2 < n_tiles)
        def _():
            start(gu_copies(s + 2, lax.rem(s + FIRST + 2, 3), True))

        @pl.when(s + 2 == n_tiles)
        def _():
            start(down_copies(0, (0, 1, 3, 4)))

        @pl.when(s + 1 == n_tiles)
        def _():
            start(down_copies(0, (2,)))
            start(down_copies(1, (0, 3, 4)))

        cols = tile_cols(s)
        xx = xa[:, pl.ds(0, d_model)]
        g = dot(xx, wbuf[2 * slot])
        u = dot(xx, wbuf[2 * slot + 1])
        gk, gr = lora(pg[kept, hot_cols], bbuf[slot, 0, hot_cols, :]), lora(pg[recv, :], bbuf[slot, 0])
        uk, ur = lora(pu[kept, hot_cols], bbuf[slot, 1, hot_cols, :]), lora(pu[recv, :], bbuf[slot, 1])
        h[kept, cols] = act(g[:half] + gk, u[:half] + uk)
        h[recv, cols] = act(g[half:] + gr, u[half:] + ur)
        add_low(slot, cols)
        return carry

    lax.fori_loop(FIRST, n_tiles, third_step, 0)
    start(down_copies(1, (1, 2)))

    pdm[kept, hot_cols] = masked(pd[kept, hot_cols].astype(BF16).astype(F32), cls_kept, hot_group, rank)
    pdm[recv, :] = masked(pd[recv, :].astype(BF16).astype(F32), cls_recv, 0, rank)

    back_rows = pl.ds(pl.multiple_of(half + me * cap, cap), cap)

    def y_remote(n, d):
        to = lax.rem(me + d, group)
        return pltpu.make_async_remote_copy(
            src_ref=xy.at[n, pl.ds(pl.multiple_of(to * cap, cap), cap)], dst_ref=xy.at[n, back_rows],
            send_sem=s2.at[n, d], recv_sem=r2.at[n, d], device_id={"data": to}, device_id_type=MESH)

    def rows_out(n, rows, low):
        y = low
        for i, (k, size) in enumerate(k_parts):
            y = dot(h[rows, pl.ds(k, size)], wbuf[down_half(n, i), pl.ds(0, size), :]) + y
        return (xa[rows, tile_cols(n)].astype(F32) + y).astype(BF16)

    def down_recv(n):
        xy[n, kept, :] = rows_out(n, recv, lora(pdm[recv, :], bbuf[down_b(n), 0]))
        for d in range(1, group):
            y_remote(n, d).start()
        xy[n, back_rows, :] = xy[n, my_block, :]

    def down_kept(n):
        y_kept[n] = rows_out(n, kept, lora(pdm[kept, hot_cols], bbuf[down_b(n), 0, hot_cols, :]))

    def out_copy(n):
        slot = lax.rem(n, 2)
        return cp(o_stage.at[slot], out_hbm.at[:, tile_cols(n)], o_sem.at[slot])

    def finish(n):
        for d in range(1, group):
            y_remote(n, d).wait_recv()
        o_stage[lax.rem(n, 2)] = (dot(unperm[:, kept], y_kept[n]) + dot(unperm[:, recv], xy[n, recv, :])).astype(BF16)
        out_copy(n).start()

    def down_step(n, carry):
        wait(down_copies(n))

        @pl.when(n > 0)
        def _():
            start(down_copies(n + 1))

        down_recv(n)
        down_kept(n)

        @pl.when(n > 0)
        def _():
            @pl.when(n > 2)
            def _():
                out_copy(n - 3).wait()
            finish(n - 1)
        return carry

    last = d_tiles - 1
    lax.fori_loop(0, last - 1, down_step, 0)
    wait(down_copies(last - 1))
    start(down_copies(last))
    down_recv(last - 1)
    out_copy(last - 4).wait()
    finish(last - 2)
    wait(down_copies(last))
    down_recv(last)
    down_kept(last - 1)
    down_kept(last)
    out_copy(last - 3).wait()
    finish(last - 1)
    out_copy(last - 2).wait()
    finish(last)
    out_copy(last - 1).wait()
    out_copy(last).wait()

    for d in range(1, group):
        x_remote(d).wait_send()

    def drain(n, carry):
        for d in range(1, group):
            y_remote(n, d).wait_send()
        return carry

    lax.fori_loop(0, d_tiles, drain, 0)


def solution(mesh):
    group = mesh.shape["data"]
    token_spec = P(("replica", "data"), None)
    store_spec = P("data", None, None)
    full_mat = P(None, None)
    full_set = P(None, None, None)
    in_specs = (token_spec, P(("replica", "data")), full_mat, full_mat, full_mat) + (store_spec,) * 6 + (P(None),) + (full_set,) * 6

    def device_step(x, adapter_id, w_gate, w_up, w_down, a_gate, b_gate, a_up, b_up, a_down, b_down, hot_ids, hot_a_gate, hot_b_gate, hot_a_up, hot_b_up, hot_a_down, hot_b_down):
        tokens, d_model = x.shape
        d_ff = w_gate.shape[1]
        n_local, _, rank = a_gate.shape
        n_hot = hot_ids.shape[0]
        cap = tokens // (2 * group)
        half = group * cap
        n_all = (n_local + n_hot) * rank
        d_tiles = d_model // TN

        def a_t(a):
            return jnp.swapaxes(a, 1, 2).reshape(a.shape[0] * rank, a.shape[1])

        def b_flat(b):
            return b.reshape(b.shape[0] * rank, b.shape[2])

        hbm = pl.BlockSpec(memory_space=pl.ANY)
        kernel = functools.partial(mlp_kernel, group, n_local, n_hot, rank, LORA_ALPHA / rank)
        return pl.pallas_call(
            kernel,
            out_shape=jax.ShapeDtypeStruct(x.shape, x.dtype),
            in_specs=[hbm] * 18,
            out_specs=hbm,
            scratch_shapes=[
                pltpu.SMEM((n_hot,), jnp.int32),
                pltpu.VMEM((1, tokens), jnp.int32),
                pltpu.VMEM((d_tiles, tokens, TN), BF16),
                pltpu.VMEM((half, d_model + 128), BF16),
                pltpu.VMEM((tokens, d_model + 128), BF16),
                pltpu.VMEM((tokens, d_ff), BF16),
                pltpu.VMEM((tokens, n_all), BF16),
                pltpu.VMEM((tokens, n_all), BF16),
                pltpu.VMEM((tokens, n_all), F32),
                pltpu.VMEM((tokens, n_all), BF16),
                pltpu.VMEM((2, n_all, d_model), BF16),
                pltpu.VMEM((6, d_model, TN), BF16),
                pltpu.VMEM((3, 2, n_all, TN), BF16),
                pltpu.VMEM((3, n_all, TN), BF16),
                pltpu.VMEM((d_tiles, half, TN), BF16),
                pltpu.VMEM((2, tokens, TN), BF16),
                pltpu.VMEM((tokens, tokens), BF16),
                pltpu.SemaphoreType.DMA((2,)),
                pltpu.SemaphoreType.DMA((d_tiles,)),
                pltpu.SemaphoreType.DMA((4,)),
                pltpu.SemaphoreType.DMA((3, 8)),
                pltpu.SemaphoreType.DMA((2, 5)),
                pltpu.SemaphoreType.DMA((2,)),
                pltpu.SemaphoreType.DMA((group,)),
                pltpu.SemaphoreType.DMA((group,)),
                pltpu.SemaphoreType.DMA((d_tiles, group)),
                pltpu.SemaphoreType.DMA((d_tiles, group)),
            ],
            compiler_params=pltpu.CompilerParams(
                collective_id=0, has_side_effects=True, vmem_limit_bytes=67043328),
        )(hot_ids, adapter_id.reshape(1, tokens), x, w_gate, w_up, w_down,
          a_t(a_gate), b_flat(b_gate), a_t(a_up), b_flat(b_up), a_t(a_down), b_flat(b_down),
          a_t(hot_a_gate), b_flat(hot_b_gate), a_t(hot_a_up), b_flat(hot_b_up), a_t(hot_a_down), b_flat(hot_b_down))

    return jax.shard_map(device_step, mesh=mesh, in_specs=in_specs, out_specs=token_spec, check_vma=False)
```

time: 136 us -> 130 us (0.956)
  Pallas kernels: 132 us -> 126 us
    pallas_call x1, Pallas kernels: 132 us -> 126 us  [device_step(): pl.pallas_call(kernel, out_shape=jax.ShapeDtypeStruct(x.shape, x.dtype),...]
where the time goes in v2:
time: 130 us
  Pallas kernels  126 us (97%)
  local copies, waits for them, and re-layouts  3.76 us (3%)
    pallas_call x1, Pallas kernels, device_step(): pl.pallas_call(kernel, out_shape=jax.ShapeDtypeStruct(x.shape, x.dtype),...  126 us
    unnamed x1, local copies, waits for them, and re-layouts  3.76 us

profile of v2, /device:TPU:0, one launch (start us, length us, event | category | flops | bytes accessed | tf_op | source)
XLA Modules:
  0.0 129.9 jit_solution(2652444084308850920)
XLA Ops:
  0.0 126.1 %shard_map.172 = bf16[512,3072]{1,0:T(8,128)(2,1)} custom-call(s32[4]{0:T(128)} %hot_hbm.1, s32[1,512]{1,0:T(1,128)} %bitcast.37, bf16[512,3072]{1,0:T(8,128)(2,1)} %x_hbm.1, bf16[3072,8192]{1,0:T(8,128)(2,1)} %wg_hbm.1, bf16[3072,8192]{1,0:T(8,128)(2,1)} %wu_hbm.1, bf16[8192,3072]{1,0:T(8,128)(2,1)} %wd_hbm.1, bf16[512,3072]{1,0:T(8,128)(2,1)} %bitcast.31, ...), custom_call_target="tpu_custom_call" | custom-call | tf_op jit(solution)/shard_map/pallas_call | solution.py:395
  126.1 3.8 %copy.20 = bf16[512,3072]{1,0:T(8,128)(2,1)} copy(bf16[512,3072]{1,0:T(8,128)(2,1)} %shard_map.172) | data formatting | bytes 6291456

commit v3 on v2

v3 whole, which is shorter than its diff:
```python
import functools

import jax
import jax.numpy as jnp
from jax import lax
from jax.experimental import pallas as pl
from jax.experimental.pallas import tpu as pltpu
from jax.sharding import PartitionSpec as P

LORA_ALPHA = 32
MESH = pl.DeviceIdType.MESH
F32 = jnp.float32
BF16 = jnp.bfloat16

TN = 512
FIRST = 10


def dot(a, b):
    return jnp.dot(a, b, preferred_element_type=F32)


def dot_t(a, b):
    return lax.dot_general(a, b, (((1,), (1,)), ((), ())), preferred_element_type=F32)


def positions(ids, hot_ids, n_hot, group, n_local, cap):
    tokens = ids.shape[1]
    kept = tokens - group * cap
    is_hot = ids < 0
    hot_idx = jnp.zeros_like(ids)
    for j in range(n_hot):
        match = ids == hot_ids[j]
        is_hot = is_hot | match
        hot_idx = jnp.where(match, j, hot_idx)
    owner = jnp.where(is_hot, group, ids // n_local)
    local = ids - (ids // n_local) * n_local
    cls = jnp.where(is_hot, n_local + hot_idx, local)
    rows = 2 * group
    kind = lax.broadcasted_iota(jnp.int32, (rows, tokens), 0)
    member = (kind == jnp.broadcast_to(owner, (rows, tokens))).astype(F32)
    before = lax.broadcasted_iota(jnp.int32, (tokens, tokens), 0) < lax.broadcasted_iota(jnp.int32, (tokens, tokens), 1)
    cum = dot(member.astype(BF16), before.astype(BF16))
    rank = jnp.sum(member * cum, axis=0, keepdims=True)
    counts = jnp.sum(member, axis=1, keepdims=True)
    sub = lax.broadcasted_iota(jnp.int32, (rows, 1), 0)
    holes = jnp.where(sub < group, cap - counts, 0.0)
    lower = lax.broadcasted_iota(jnp.int32, (rows, rows), 1) < lax.broadcasted_iota(jnp.int32, (rows, rows), 0)
    hole_start = dot(lower.astype(BF16), jnp.broadcast_to(holes, (rows, 128)).astype(BF16))[:, 0:1]
    spill = jnp.broadcast_to(rank - kept, (rows, tokens))
    takes = (spill >= hole_start) & (spill < hole_start + holes)
    base = kept + cap * sub.astype(F32) + counts - hole_start
    filled = jnp.sum(jnp.where(takes, base + spill, 0.0), axis=0, keepdims=True)
    own = kept + cap * owner.astype(F32) + rank
    pos = jnp.where(is_hot, jnp.where(rank < kept, rank, filled), own)
    return pos, cls.astype(F32)


def masked(low, cls, first_group, rank):
    per = 128 // rank
    lane = lax.broadcasted_iota(jnp.int32, (low.shape[0], 128), 1) // rank
    parts = []
    for k in range(low.shape[1] // 128):
        here = (lane + per * (first_group + k)).astype(F32) == cls
        parts.append(jnp.where(here, low[:, k * 128:(k + 1) * 128], 0.0).astype(BF16))
    return jnp.concatenate(parts, axis=1)


def mlp_kernel(group, n_local, n_hot, rank, scale,
               hot_hbm, ids_hbm, x_hbm, wg_hbm, wu_hbm, wd_hbm,
               ag_hbm, bg_hbm, au_hbm, bu_hbm, ad_hbm, bd_hbm,
               hag_hbm, hbg_hbm, hau_hbm, hbu_hbm, had_hbm, hbd_hbm,
               y_hbm, unperm_hbm,
               hot_ids, ids, xy, xsend, xa, h, pg, pu, pd, pdm, wbuf, bbuf, adbuf, unperm,
               id_sem, x_sem, at_sem, w_sem, ad_sem, d_sem, y_sem, p_sem, s1, r1, s2, r2):
    me = lax.axis_index("data")
    tokens, d_model = x_hbm.shape
    d_ff = wg_hbm.shape[1]
    cap = tokens // (2 * group)
    half = group * cap
    n_own = n_local * rank
    n_hr = n_hot * rank
    n_all = n_own + n_hr
    n_tiles = d_ff // TN
    d_tiles = d_model // TN
    kept = pl.ds(0, half)
    recv = pl.ds(half, half)
    own_cols = pl.ds(0, n_own)
    hot_cols = pl.ds(n_own, n_hr)
    hot_group = n_own // 128
    lead = (FIRST - 1 + n_tiles) % 3
    k_parts = [(k, min(d_model, d_ff - k)) for k in range(0, d_ff, d_model)]
    assert len(k_parts) == 3

    def cp(src, dst, sem):
        return pltpu.make_async_copy(src, dst, sem)

    def tile_cols(tile):
        return pl.ds(tile * TN if isinstance(tile, int) else pl.multiple_of(tile * TN, TN), TN)

    def gu_base(tile, slot):
        cols = tile_cols(tile)
        return [
            cp(wg_hbm.at[:, cols], wbuf.at[2 * slot], w_sem.at[slot, 0]),
            cp(wu_hbm.at[:, cols], wbuf.at[2 * slot + 1], w_sem.at[slot, 1]),
            cp(hbg_hbm.at[:, cols], bbuf.at[slot, 0, hot_cols], w_sem.at[slot, 2]),
            cp(hbu_hbm.at[:, cols], bbuf.at[slot, 1, hot_cols], w_sem.at[slot, 3]),
        ]

    def gu_extra(tile, slot, ad_slot):
        cols = tile_cols(tile)
        return [
            cp(bg_hbm.at[:, cols], bbuf.at[slot, 0, own_cols], w_sem.at[slot, 4]),
            cp(bu_hbm.at[:, cols], bbuf.at[slot, 1, own_cols], w_sem.at[slot, 5]),
            cp(ad_hbm.at[:, cols], adbuf.at[ad_slot, own_cols], ad_sem.at[ad_slot, 0]),
            cp(had_hbm.at[:, cols], adbuf.at[ad_slot, hot_cols], ad_sem.at[ad_slot, 1]),
        ]

    def ring(s):
        return lax.rem(s + FIRST - 1, 3)

    def gu_full(tile, s):
        return gu_base(tile, ring(s)) + gu_extra(tile, ring(s), lax.rem(s, 4))

    def a_view(i, c, first, size):
        index = i * d_tiles + c
        per = d_model // n_all
        return wbuf.at[6 + index // per, pl.ds((index % per) * n_all + first, size)]

    def a_copies(i, src, first, size, side):
        return [cp(src.at[:, pl.ds(c * TN, TN)], a_view(i, c, first, size), at_sem.at[2 * side + i, c]) for c in range(d_tiles)]

    def down_half(n, i):
        k = lax.rem(n, 3)
        return jnp.where(k == 0, 6 + i, lax.rem(2 * lead + 3 * (k + 1) + i, 6))

    def down_b(n):
        k = lax.rem(n, 3)
        return lax.rem(lead + k // 2, 3), lax.rem(k, 2)

    def down_copies(n, pieces=(0, 1, 2, 3, 4)):
        cols = tile_cols(n)
        out = []
        for i in pieces:
            if i < 3:
                k, size = k_parts[i]
                src, dst = wd_hbm.at[pl.ds(k, size), cols], wbuf.at[down_half(n, i), pl.ds(0, size)]
            elif i == 3:
                src, dst = bd_hbm.at[:, cols], bbuf.at[down_b(n)[0], down_b(n)[1], own_cols]
            else:
                src, dst = hbd_hbm.at[:, cols], bbuf.at[down_b(n)[0], down_b(n)[1], hot_cols]
            out.append(cp(src, dst, d_sem.at[lax.rem(n, 3), i]))
        return out

    def start(copies):
        for c in copies:
            c.start()

    def wait(copies):
        for c in copies:
            c.wait()

    id_copies = [cp(ids_hbm, ids, id_sem.at[0]), cp(hot_hbm, hot_ids, id_sem.at[1])]
    x_copies = [cp(x_hbm.at[:, pl.ds(n * TN, TN)], xy.at[n], x_sem.at[n]) for n in range(d_tiles)]
    a_hot = a_copies(0, hag_hbm, n_own, n_hr, 0) + a_copies(1, hau_hbm, n_own, n_hr, 0)
    a_own = a_copies(0, ag_hbm, 0, n_own, 1) + a_copies(1, au_hbm, 0, n_own, 1)
    start(id_copies)
    start(x_copies)
    start(a_hot)
    start(gu_base(0, 0))
    start(gu_base(1, 1))

    barrier = pltpu.get_barrier_semaphore()
    for d in range(1, group):
        pl.semaphore_signal(barrier, inc=1, device_id={"data": lax.rem(me + d, group)}, device_id_type=MESH)

    wait(id_copies)
    pos, cls = positions(ids[...], hot_ids, n_hot, group, n_local, cap)
    place = jnp.broadcast_to(pos.astype(jnp.int32), (tokens, tokens))
    perm = (place == lax.broadcasted_iota(jnp.int32, (tokens, tokens), 0)).astype(BF16)
    cls_rows = dot_t(perm, jnp.broadcast_to(cls, (128, tokens)).astype(BF16)).astype(BF16)
    xsend[:, pl.ds(d_model, 128)] = cls_rows[half:]
    xa[kept, pl.ds(d_model, 128)] = cls_rows[:half]
    wait(x_copies)
    for n in range(d_tiles):
        cols = pl.ds(n * TN, TN)
        moved = dot(perm, xy[n])
        xsend[:, cols] = moved[half:].astype(BF16)
        xa[kept, cols] = moved[:half].astype(BF16)

    pl.semaphore_wait(barrier, group - 1)
    my_block = pl.ds(pl.multiple_of(me * cap, cap), cap)
    my_rows = pl.ds(pl.multiple_of(half + me * cap, cap), cap)

    def x_remote(d):
        to = lax.rem(me + d, group)
        return pltpu.make_async_remote_copy(
            src_ref=xsend.at[pl.ds(pl.multiple_of(to * cap, cap), cap)], dst_ref=xa.at[my_rows],
            send_sem=s1.at[d], recv_sem=r1.at[d], device_id={"data": to}, device_id_type=MESH)

    for d in range(1, group):
        x_remote(d).start()
    wait(a_hot)
    xa[my_rows, :] = xsend[my_block, :]
    pos_col = jnp.transpose(jnp.broadcast_to(pos, (128, tokens)))[:, 0:1].astype(jnp.int32)
    unperm[...] = (pos_col == lax.broadcasted_iota(jnp.int32, (tokens, tokens), 1)).astype(BF16)

    def delta(low, b):
        return (scale * dot(low, b)).astype(BF16)

    def act(g, u, dg, du):
        g = g + dg.astype(F32)
        u = u + du.astype(F32)
        return (g * jax.nn.sigmoid(g) * u).astype(BF16)

    def low_rank(rows, first, size):
        low = [None, None]
        for c in range(d_tiles):
            for i in range(2):
                part = dot_t(xa[rows, pl.ds(c * TN, TN)], a_view(i, c, first, size)[...])
                low[i] = part if low[i] is None else low[i] + part
        return low

    def masked_bf16(low, cls, first_group):
        return masked(low.astype(BF16).astype(F32), cls, first_group, rank)

    cls_kept = xa[kept, pl.ds(d_model, 128)].astype(F32)
    low_g, low_u = low_rank(kept, n_own, n_hr)
    pg[kept, hot_cols] = masked_bf16(low_g, cls_kept, hot_group)
    pu[kept, hot_cols] = masked_bf16(low_u, cls_kept, hot_group)

    def first_step(s, carry):
        slot = lax.rem(s, 3)
        ahead = lax.rem(s + 2, 3)
        wait(gu_base(s, slot))

        @pl.when(s + 2 < FIRST)
        def _():
            start(gu_base(s + 2, ahead))

        @pl.when(s + 3 == FIRST)
        def _():
            start(gu_extra(FIRST - 1, ahead, 0))

        @pl.when(s + 2 >= FIRST)
        def _():
            start(gu_full(s + 2 - FIRST, s + 3 - FIRST))

        @pl.when(s == 1)
        def _():
            start(a_own)

        xk = xa[kept, pl.ds(0, d_model)]
        dg = delta(pg[kept, hot_cols], bbuf[slot, 0, hot_cols, :])
        du = delta(pu[kept, hot_cols], bbuf[slot, 1, hot_cols, :])
        h[kept, tile_cols(s)] = act(dot(xk, wbuf[2 * slot]), dot(xk, wbuf[2 * slot + 1]), dg, du)
        return carry

    lax.fori_loop(0, FIRST, first_step, 0)

    cp(unperm, unperm_hbm, p_sem).start()
    wait(a_own)
    for d in range(1, group):
        x_remote(d).wait_recv()
    cls_recv = xa[recv, pl.ds(d_model, 128)].astype(F32)
    low_g, low_u = low_rank(recv, 0, n_all)
    pg[recv, :] = masked_bf16(low_g, cls_recv, 0)
    pu[recv, :] = masked_bf16(low_u, cls_recv, 0)
    pd[...] = jnp.zeros_like(pd)

    def add_low(tile, ad_slot):
        cols = tile_cols(tile)
        low_kept = dot_t(h[kept, cols], adbuf[ad_slot, hot_cols, :])
        low_recv = dot_t(h[recv, cols], adbuf[ad_slot])
        pd[kept, hot_cols] += low_kept
        pd[recv, :] += low_recv

    def recv_tile(tile, slot, between):
        xr = xa[recv, pl.ds(0, d_model)]
        dg, du = delta(pg[recv, :], bbuf[slot, 0]), delta(pu[recv, :], bbuf[slot, 1])
        g, u = dot(xr, wbuf[2 * slot]), dot(xr, wbuf[2 * slot + 1])
        between()
        h[recv, tile_cols(tile)] = act(g, u, dg, du)

    wait(gu_extra(FIRST - 1, (FIRST - 1) % 3, 0))
    recv_tile(FIRST - 1, (FIRST - 1) % 3, lambda: None)

    def second_step(s, carry):
        wait(gu_full(s - 1, s))
        start(gu_full(jnp.where(s + 2 < FIRST, s + 1, s + 2), s + 2))
        recv_tile(s - 1, ring(s), lambda: add_low(jnp.where(s == 1, FIRST - 1, s - 2), lax.rem(s + 3, 4)))
        return carry

    lax.fori_loop(1, FIRST, second_step, 0)

    def third_step(s, carry):
        slot = ring(s)
        wait(gu_full(s, s))

        @pl.when(s + 2 < n_tiles)
        def _():
            start(gu_full(s + 2, s + 2))

        @pl.when(s == FIRST)
        def _():
            start(down_copies(0, (0, 1, 2)))

        @pl.when(s + 2 == n_tiles)
        def _():
            start(down_copies(0, (3, 4)) + down_copies(1, (0, 1, 3, 4)))

        @pl.when(s + 1 == n_tiles)
        def _():
            start(down_copies(1, (2,)) + down_copies(2, (0, 3, 4)))

        xx = xa[:, pl.ds(0, d_model)]
        dgk = delta(pg[kept, hot_cols], bbuf[slot, 0, hot_cols, :])
        dgr = delta(pg[recv, :], bbuf[slot, 0])
        duk = delta(pu[kept, hot_cols], bbuf[slot, 1, hot_cols, :])
        dur = delta(pu[recv, :], bbuf[slot, 1])
        g, u = dot(xx, wbuf[2 * slot]), dot(xx, wbuf[2 * slot + 1])
        add_low(jnp.where(s == FIRST, FIRST - 2, s - 1), lax.rem(s + 3, 4))
        h[kept, tile_cols(s)] = act(g[:half], u[:half], dgk, duk)
        h[recv, tile_cols(s)] = act(g[half:], u[half:], dgr, dur)
        return carry

    lax.fori_loop(FIRST, n_tiles, third_step, 0)
    start(down_copies(2, (1, 2)))
    add_low(n_tiles - 1, (n_tiles - 1) % 4)

    pdm[kept, hot_cols] = masked_bf16(pd[kept, hot_cols], cls_kept, hot_group)
    pdm[recv, :] = masked_bf16(pd[recv, :], cls_recv, 0)

    def y_remote(n, d):
        to = lax.rem(me + d, group)
        return pltpu.make_async_remote_copy(
            src_ref=xy.at[n, pl.ds(pl.multiple_of(to * cap, cap), cap)], dst_ref=y_hbm.at[my_rows, tile_cols(n)],
            send_sem=s2.at[n, d], recv_sem=r2.at[n, d], device_id={"data": to}, device_id_type=MESH)

    def y_local(n):
        return [cp(xy.at[n, recv], y_hbm.at[kept, tile_cols(n)], y_sem.at[n, 0])]

    def y_self(n):
        return [cp(xy.at[n, my_block], y_hbm.at[my_rows, tile_cols(n)], y_sem.at[n, 1])]

    def rows_out(n, rows, low):
        y = low
        for i, (k, size) in enumerate(k_parts):
            y = dot(h[rows, pl.ds(k, size)], wbuf[down_half(n, i), pl.ds(0, size), :]) + y
        return (xa[rows, tile_cols(n)].astype(F32) + y).astype(BF16)

    def down_recv(n):
        slot, part = down_b(n)
        xy[n, kept, :] = rows_out(n, recv, delta(pdm[recv, :], bbuf[slot, part]).astype(F32))

    def down_kept(n):
        slot, part = down_b(n)
        xy[n, recv, :] = rows_out(n, kept, delta(pdm[kept, hot_cols], bbuf[slot, part, hot_cols, :]).astype(F32))

    def send_back(n):
        for d in range(1, group):
            y_remote(n, d).start()
        start(y_self(n))

    def down_step(n, carry):
        wait(down_copies(n))

        @pl.when(n > 0)
        def _():
            start(down_copies(n + 2))

        down_recv(n)
        down_kept(n)
        send_back(n)
        start(y_local(n))
        return carry

    last = d_tiles - 1
    lax.fori_loop(0, last - 1, down_step, 0)
    wait(down_copies(last - 1))
    wait(down_copies(last))
    down_recv(last - 1)
    send_back(last - 1)
    down_recv(last)
    send_back(last)
    down_kept(last - 1)
    down_kept(last)
    start(y_local(last - 1) + y_local(last))

    for d in range(1, group):
        x_remote(d).wait_send()
    cp(unperm, unperm_hbm, p_sem).wait()

    def drain(n, carry):
        wait(y_self(n) + y_local(n))
        for d in range(1, group):
            y_remote(n, d).wait_send()
            y_remote(n, d).wait_recv()
        return carry

    lax.fori_loop(0, d_tiles, drain, 0)


def place_kernel(y_hbm, unperm_hbm, out_hbm, y, unperm, out, y_sem, p_sem, o_sem):
    tiles = y.shape[0]

    def y_copy(n):
        return pltpu.make_async_copy(y_hbm.at[:, pl.ds(n * TN, TN)], y.at[n], y_sem.at[n])

    def o_copy(n):
        return pltpu.make_async_copy(out.at[n], out_hbm.at[:, pl.ds(n * TN, TN)], o_sem.at[n])

    p_copy = pltpu.make_async_copy(unperm_hbm, unperm, p_sem)
    p_copy.start()
    for n in range(tiles):
        y_copy(n).start()
    p_copy.wait()
    for n in range(tiles):
        y_copy(n).wait()
        out[n] = dot(unperm[...], y[n]).astype(BF16)
        o_copy(n).start()
    for n in range(tiles):
        o_copy(n).wait()


def solution(mesh):
    group = mesh.shape["data"]
    token_spec = P(("replica", "data"), None)
    store_spec = P("data", None, None)
    full_mat = P(None, None)
    full_set = P(None, None, None)
    in_specs = (token_spec, P(("replica", "data")), full_mat, full_mat, full_mat) + (store_spec,) * 6 + (P(None),) + (full_set,) * 6

    def device_step(x, adapter_id, w_gate, w_up, w_down, a_gate, b_gate, a_up, b_up, a_down, b_down, hot_ids, hot_a_gate, hot_b_gate, hot_a_up, hot_b_up, hot_a_down, hot_b_down):
        tokens, d_model = x.shape
        d_ff = w_gate.shape[1]
        n_local, _, rank = a_gate.shape
        n_hot = hot_ids.shape[0]
        cap = tokens // (2 * group)
        half = group * cap
        n_all = (n_local + n_hot) * rank
        d_tiles = d_model // TN

        def a_t(a):
            return jnp.swapaxes(a, 1, 2).reshape(a.shape[0] * rank, a.shape[1])

        def b_flat(b):
            return b.reshape(b.shape[0] * rank, b.shape[2])

        hbm = pl.BlockSpec(memory_space=pl.ANY)
        kernel = functools.partial(mlp_kernel, group, n_local, n_hot, rank, LORA_ALPHA / rank)
        y, unperm = pl.pallas_call(
            kernel,
            out_shape=(jax.ShapeDtypeStruct(x.shape, x.dtype), jax.ShapeDtypeStruct((tokens, tokens), BF16)),
            in_specs=[hbm] * 18,
            out_specs=(hbm, hbm),
            scratch_shapes=[
                pltpu.SMEM((n_hot,), jnp.int32),
                pltpu.VMEM((1, tokens), jnp.int32),
                pltpu.VMEM((d_tiles, tokens, TN), BF16),
                pltpu.VMEM((half, d_model + 128), BF16),
                pltpu.VMEM((tokens, d_model + 128), BF16),
                pltpu.VMEM((tokens, d_ff), BF16),
                pltpu.VMEM((tokens, n_all), BF16),
                pltpu.VMEM((tokens, n_all), BF16),
                pltpu.VMEM((tokens, n_all), F32),
                pltpu.VMEM((tokens, n_all), BF16),
                pltpu.VMEM((9, d_model, TN), BF16),
                pltpu.VMEM((3, 2, n_all, TN), BF16),
                pltpu.VMEM((4, n_all, TN), BF16),
                pltpu.VMEM((tokens, tokens), BF16),
                pltpu.SemaphoreType.DMA((2,)),
                pltpu.SemaphoreType.DMA((d_tiles,)),
                pltpu.SemaphoreType.DMA((4, d_tiles)),
                pltpu.SemaphoreType.DMA((3, 6)),
                pltpu.SemaphoreType.DMA((4, 2)),
                pltpu.SemaphoreType.DMA((3, 5)),
                pltpu.SemaphoreType.DMA((d_tiles, 2)),
                pltpu.SemaphoreType.DMA,
                pltpu.SemaphoreType.DMA((group,)),
                pltpu.SemaphoreType.DMA((group,)),
                pltpu.SemaphoreType.DMA((d_tiles, group)),
                pltpu.SemaphoreType.DMA((d_tiles, group)),
            ],
            compiler_params=pltpu.CompilerParams(
                collective_id=0, has_side_effects=True, vmem_limit_bytes=67043328),
        )(hot_ids, adapter_id.reshape(1, tokens), x, w_gate, w_up, w_down,
          a_t(a_gate), b_flat(b_gate), a_t(a_up), b_flat(b_up), a_t(a_down), b_flat(b_down),
          a_t(hot_a_gate), b_flat(hot_b_gate), a_t(hot_a_up), b_flat(hot_b_up), a_t(hot_a_down), b_flat(hot_b_down))
        return pl.pallas_call(
            place_kernel,
            out_shape=jax.ShapeDtypeStruct(x.shape, x.dtype),
            in_specs=[hbm] * 2,
            out_specs=hbm,
            scratch_shapes=[
                pltpu.VMEM((d_tiles, tokens, TN), BF16),
                pltpu.VMEM((tokens, tokens), BF16),
                pltpu.VMEM((d_tiles, tokens, TN), BF16),
                pltpu.SemaphoreType.DMA((d_tiles,)),
                pltpu.SemaphoreType.DMA,
                pltpu.SemaphoreType.DMA((d_tiles,)),
            ],
        )(y, unperm)

    return jax.shard_map(device_step, mesh=mesh, in_specs=in_specs, out_specs=token_spec, check_vma=False)
```

time: 130 us -> 125 us (0.962)
  local copies, waits for them, and re-layouts: 3.76 us -> 0 us
    unnamed x1 -> x0, local copies, waits for them, and re-layouts: 3.76 us -> none
    pallas_call x1 -> x2, Pallas kernels: 126 us -> 125 us  [the longest x1 119 us: device_step(): pl.pallas_call(kernel, out_shape=(jax.ShapeDtypeStruct(x.shape, x.dtype),...]
where the time goes in v3:
time: 125 us
  Pallas kernels  125 us (100%)
    pallas_call x1, Pallas kernels, device_step(): pl.pallas_call(kernel, out_shape=(jax.ShapeDtypeStruct(x.shape, x.dtype),...  119 us
    pallas_call x1, Pallas kernels, device_step(): pl.pallas_call(place_kernel, out_shape=jax.ShapeDtypeStruct(x.shape, x.dt...  5.4 us

profile of v3, /device:TPU:0, one launch (start us, length us, event | category | flops | bytes accessed | tf_op | source)
XLA Modules:
  0.0 125.0 jit_solution(11663590406557158141)
XLA Ops:
  0.0 119.4 %shard_map.172 = (bf16[512,3072]{1,0:T(8,128)(2,1)}, bf16[512,512]{1,0:T(8,128)(2,1)}) custom-call(s32[4]{0:T(128)} %hot_hbm.1, s32[1,512]{1,0:T(1,128)} %bitcast.37, bf16[512,3072]{1,0:T(8,128)(2,1)} %x_hbm.1, bf16[3072,8192]{1,0:T(8,128)(2,1)} %wg_hbm.1, bf16[3072,8192]{1,0:T(8,128)(2,1)} %wu_hbm.1, bf16[8192,3072]{1,0:T(8,128)(2,1)} %wd_hbm.1, ...), custom_call_target="tpu_custom_call" | custom-call | tf_op jit(solution)/shard_map/pallas_call | solution.py:452
  119.4 5.4 %shard_map.173 = bf16[512,3072]{1,0:T(8,128)(2,1)} custom-call(bf16[512,3072]{1,0:T(8,128)(2,1)} %get-tuple-element.7.y_hbm, bf16[512,512]{1,0:T(8,128)(2,1)} %get-tuple-element.8.unperm_hbm), custom_call_target="tpu_custom_call" | custom-call | tf_op jit(solution)/shard_map/pallas_call | solution.py:490

commit v4 on v3

--- a/solution.py
+++ b/solution.py
@@ -13,7 +13,7 @@
 BF16 = jnp.bfloat16
 
 TN = 512
-FIRST = 10
+FIRST = 8
 
 
 def dot(a, b):
@@ -24,7 +24,12 @@
     return lax.dot_general(a, b, (((1,), (1,)), ((), ())), preferred_element_type=F32)
 
 
-def positions(ids, hot_ids, n_hot, group, n_local, cap):
+def earlier(tokens):
+    row = lax.broadcasted_iota(jnp.int32, (tokens, tokens), 0)
+    return (row < lax.broadcasted_iota(jnp.int32, (tokens, tokens), 1)).astype(BF16)
+
+
+def positions(ids, hot_ids, before, n_hot, group, n_local, cap):
     tokens = ids.shape[1]
     kept = tokens - group * cap
     is_hot = ids < 0
@@ -39,8 +44,7 @@
     rows = 2 * group
     kind = lax.broadcasted_iota(jnp.int32, (rows, tokens), 0)
     member = (kind == jnp.broadcast_to(owner, (rows, tokens))).astype(F32)
-    before = lax.broadcasted_iota(jnp.int32, (tokens, tokens), 0) < lax.broadcasted_iota(jnp.int32, (tokens, tokens), 1)
-    cum = dot(member.astype(BF16), before.astype(BF16))
+    cum = dot(member.astype(BF16), before)
     rank = jnp.sum(member * cum, axis=0, keepdims=True)
     counts = jnp.sum(member, axis=1, keepdims=True)
     sub = lax.broadcasted_iota(jnp.int32, (rows, 1), 0)
@@ -90,7 +94,7 @@
     hot_group = n_own // 128
     lead = (FIRST - 1 + n_tiles) % 3
     k_parts = [(k, min(d_model, d_ff - k)) for k in range(0, d_ff, d_model)]
-    assert len(k_parts) == 3
+    assert len(k_parts) == 3 and n_tiles == 2 * FIRST
 
     def cp(src, dst, sem):
         return pltpu.make_async_copy(src, dst, sem)
@@ -174,8 +178,9 @@
     for d in range(1, group):
         pl.semaphore_signal(barrier, inc=1, device_id={"data": lax.rem(me + d, group)}, device_id_type=MESH)
 
+    before = earlier(tokens)
     wait(id_copies)
-    pos, cls = positions(ids[...], hot_ids, n_hot, group, n_local, cap)
+    pos, cls = positions(ids[...], hot_ids, before, n_hot, group, n_local, cap)
     place = jnp.broadcast_to(pos.astype(jnp.int32), (tokens, tokens))
     perm = (place == lax.broadcasted_iota(jnp.int32, (tokens, tokens), 0)).astype(BF16)
     cls_rows = dot_t(perm, jnp.broadcast_to(cls, (128, tokens)).astype(BF16)).astype(BF16)
@@ -183,10 +188,7 @@
     xa[kept, pl.ds(d_model, 128)] = cls_rows[:half]
     wait(x_copies)
     for n in range(d_tiles):
-        cols = pl.ds(n * TN, TN)
-        moved = dot(perm, xy[n])
-        xsend[:, cols] = moved[half:].astype(BF16)
-        xa[kept, cols] = moved[:half].astype(BF16)
+        xsend[:, pl.ds(n * TN, TN)] = dot(perm[half:], xy[n]).astype(BF16)
 
     pl.semaphore_wait(barrier, group - 1)
     my_block = pl.ds(pl.multiple_of(me * cap, cap), cap)
@@ -196,10 +198,17 @@
         to = lax.rem(me + d, group)
         return pltpu.make_async_remote_copy(
             src_ref=xsend.at[pl.ds(pl.multiple_of(to * cap, cap), cap)], dst_ref=xa.at[my_rows],
-            send_sem=s1.at[d], recv_sem=r1.at[d], device_id={"data": to}, device_id_type=MESH)
+            send_sem=s1, recv_sem=r1, device_id={"data": to}, device_id_type=MESH)
+
+    others = (group - 1) * cap
+    x_all = pltpu.make_async_remote_copy(
+        src_ref=xsend.at[pl.ds(0, others)], dst_ref=xa.at[pl.ds(half, others)],
+        send_sem=s1, recv_sem=r1, device_id={"data": lax.rem(me + 1, group)}, device_id_type=MESH)
 
     for d in range(1, group):
         x_remote(d).start()
+    for n in range(d_tiles):
+        xa[kept, pl.ds(n * TN, TN)] = dot(perm[:half], xy[n]).astype(BF16)
     wait(a_hot)
     xa[my_rows, :] = xsend[my_block, :]
     pos_col = jnp.transpose(jnp.broadcast_to(pos, (128, tokens)))[:, 0:1].astype(jnp.int32)
@@ -244,7 +253,7 @@
 
         @pl.when(s + 2 >= FIRST)
         def _():
-            start(gu_full(s + 2 - FIRST, s + 3 - FIRST))
+            start(gu_full(jnp.where(s + 2 == FIRST, FIRST, 0), s + 3 - FIRST))
 
         @pl.when(s == 1)
         def _():
@@ -260,8 +269,7 @@
 
     cp(unperm, unperm_hbm, p_sem).start()
     wait(a_own)
-    for d in range(1, group):
-        x_remote(d).wait_recv()
+    x_all.wait_recv()
     cls_recv = xa[recv, pl.ds(d_model, 128)].astype(F32)
     low_g, low_u = low_rank(recv, 0, n_all)
     pg[recv, :] = masked_bf16(low_g, cls_recv, 0)
@@ -282,49 +290,48 @@
         between()
         h[recv, tile_cols(tile)] = act(g, u, dg, du)
 
-    wait(gu_extra(FIRST - 1, (FIRST - 1) % 3, 0))
-    recv_tile(FIRST - 1, (FIRST - 1) % 3, lambda: None)
-
-    def second_step(s, carry):
-        wait(gu_full(s - 1, s))
-        start(gu_full(jnp.where(s + 2 < FIRST, s + 1, s + 2), s + 2))
-        recv_tile(s - 1, ring(s), lambda: add_low(jnp.where(s == 1, FIRST - 1, s - 2), lax.rem(s + 3, 4)))
-        return carry
-
-    lax.fori_loop(1, FIRST, second_step, 0)
-
-    def third_step(s, carry):
-        slot = ring(s)
-        wait(gu_full(s, s))
-
-        @pl.when(s + 2 < n_tiles)
-        def _():
-            start(gu_full(s + 2, s + 2))
-
-        @pl.when(s == FIRST)
-        def _():
-            start(down_copies(0, (0, 1, 2)))
-
-        @pl.when(s + 2 == n_tiles)
-        def _():
-            start(down_copies(0, (3, 4)) + down_copies(1, (0, 1, 3, 4)))
-
-        @pl.when(s + 1 == n_tiles)
-        def _():
-            start(down_copies(1, (2,)) + down_copies(2, (0, 3, 4)))
-
+    def all_tile(tile, slot, between):
         xx = xa[:, pl.ds(0, d_model)]
+        g, u = dot(xx, wbuf[2 * slot]), dot(xx, wbuf[2 * slot + 1])
         dgk = delta(pg[kept, hot_cols], bbuf[slot, 0, hot_cols, :])
         dgr = delta(pg[recv, :], bbuf[slot, 0])
         duk = delta(pu[kept, hot_cols], bbuf[slot, 1, hot_cols, :])
         dur = delta(pu[recv, :], bbuf[slot, 1])
-        g, u = dot(xx, wbuf[2 * slot]), dot(xx, wbuf[2 * slot + 1])
-        add_low(jnp.where(s == FIRST, FIRST - 2, s - 1), lax.rem(s + 3, 4))
-        h[kept, tile_cols(s)] = act(g[:half], u[:half], dgk, duk)
-        h[recv, tile_cols(s)] = act(g[half:], u[half:], dgr, dur)
+        between()
+        h[kept, tile_cols(tile)] = act(g[:half], u[:half], dgk, duk)
+        h[recv, tile_cols(tile)] = act(g[half:], u[half:], dgr, dur)
+
+    wait(gu_extra(FIRST - 1, (FIRST - 1) % 3, 0))
+    recv_tile(FIRST - 1, (FIRST - 1) % 3, lambda: None)
+
+    def second_step(p, carry):
+        s = 2 * p + 1
+        wait(gu_full(FIRST + p, s))
+        start(gu_full(FIRST + p + 1, s + 2))
+
+        @pl.when(p == 1)
+        def _():
+            start(down_copies(0, (0, 1, 2)))
+
+        all_tile(FIRST + p, ring(s), lambda: add_low(jnp.where(p == 0, FIRST - 1, p - 1), lax.rem(s + 3, 4)))
+        wait(gu_full(p, s + 1))
+
+        @pl.when(p + 2 < FIRST)
+        def _():
+            start(gu_full(p + 1, s + 3))
+
+        @pl.when(p + 2 == FIRST)
+        def _():
+            start(down_copies(0, (3, 4)) + down_copies(1, (0, 1, 3, 4)))
+
+        recv_tile(p, ring(s + 1), lambda: add_low(FIRST + p, lax.rem(s, 4)))
         return carry
 
-    lax.fori_loop(FIRST, n_tiles, third_step, 0)
+    lax.fori_loop(0, FIRST - 1, second_step, 0)
+    s_last = n_tiles - 1
+    wait(gu_full(n_tiles - 1, s_last))
+    start(down_copies(1, (2,)) + down_copies(2, (0, 3, 4)))
+    all_tile(n_tiles - 1, (s_last + FIRST - 1) % 3, lambda: add_low(FIRST - 2, (s_last + 3) % 4))
     start(down_copies(2, (1, 2)))
     add_low(n_tiles - 1, (n_tiles - 1) % 4)
 
@@ -335,7 +342,12 @@
         to = lax.rem(me + d, group)
         return pltpu.make_async_remote_copy(
             src_ref=xy.at[n, pl.ds(pl.multiple_of(to * cap, cap), cap)], dst_ref=y_hbm.at[my_rows, tile_cols(n)],
-            send_sem=s2.at[n, d], recv_sem=r2.at[n, d], device_id={"data": to}, device_id_type=MESH)
+            send_sem=s2.at[n], recv_sem=r2.at[n], device_id={"data": to}, device_id_type=MESH)
+
+    def y_all(n):
+        return pltpu.make_async_remote_copy(
+            src_ref=xy.at[n, pl.ds(0, others)], dst_ref=y_hbm.at[pl.ds(half, others), tile_cols(n)],
+            send_sem=s2.at[n], recv_sem=r2.at[n], device_id={"data": lax.rem(me + 1, group)}, device_id_type=MESH)
 
     def y_local(n):
         return [cp(xy.at[n, recv], y_hbm.at[kept, tile_cols(n)], y_sem.at[n, 0])]
@@ -375,30 +387,30 @@
         start(y_local(n))
         return carry
 
-    last = d_tiles - 1
-    lax.fori_loop(0, last - 1, down_step, 0)
-    wait(down_copies(last - 1))
-    wait(down_copies(last))
-    down_recv(last - 1)
-    send_back(last - 1)
-    down_recv(last)
-    send_back(last)
-    down_kept(last - 1)
-    down_kept(last)
-    start(y_local(last - 1) + y_local(last))
-
-    for d in range(1, group):
-        x_remote(d).wait_send()
+    early = d_tiles - 3
+    lax.fori_loop(0, early, down_step, 0)
+    start(down_copies(d_tiles - 1))
+
+    def late_recv(n, carry):
+        wait(down_copies(n))
+        down_recv(n)
+        send_back(n)
+        return carry
+
+    def late_kept(n, carry):
+        down_kept(n)
+        start(y_local(n))
+        return carry
+
+    lax.fori_loop(early, d_tiles, late_recv, 0)
+    lax.fori_loop(early, d_tiles, late_kept, 0)
+
+    x_all.wait_send()
     cp(unperm, unperm_hbm, p_sem).wait()
-
-    def drain(n, carry):
+    for n in range(d_tiles):
         wait(y_self(n) + y_local(n))
-        for d in range(1, group):
-            y_remote(n, d).wait_send()
-            y_remote(n, d).wait_recv()
-        return carry
-
-    lax.fori_loop(0, d_tiles, drain, 0)
+        y_all(n).wait_send()
+        y_all(n).wait_recv()
 
 
 def place_kernel(y_hbm, unperm_hbm, out_hbm, y, unperm, out, y_sem, p_sem, o_sem):
@@ -415,10 +427,13 @@
     for n in range(tiles):
         y_copy(n).start()
     p_copy.wait()
-    for n in range(tiles):
-        y_copy(n).wait()
-        out[n] = dot(unperm[...], y[n]).astype(BF16)
-        o_copy(n).start()
+    for group in ((0,), (1, 2), tuple(range(3, tiles))):
+        for n in group:
+            y_copy(n).wait()
+        for n in group:
+            out[n] = dot(unperm[...], y[n]).astype(BF16)
+        for n in group:
+            o_copy(n).start()
     for n in range(tiles):
         o_copy(n).wait()
 
@@ -477,10 +492,10 @@
                 pltpu.SemaphoreType.DMA((3, 5)),
                 pltpu.SemaphoreType.DMA((d_tiles, 2)),
                 pltpu.SemaphoreType.DMA,
-                pltpu.SemaphoreType.DMA((group,)),
-                pltpu.SemaphoreType.DMA((group,)),
-                pltpu.SemaphoreType.DMA((d_tiles, group)),
-                pltpu.SemaphoreType.DMA((d_tiles, group)),
+                pltpu.SemaphoreType.DMA,
+                pltpu.SemaphoreType.DMA,
+                pltpu.SemaphoreType.DMA((d_tiles,)),
+                pltpu.SemaphoreType.DMA((d_tiles,)),
             ],
             compiler_params=pltpu.CompilerParams(
                 collective_id=0, has_side_effects=True, vmem_limit_bytes=67043328),

time: 125 us -> 124 us (level); the launches traced: 125 us -> 123 us
  Pallas kernels: 125 us -> 122 us
    pallas_call x1, Pallas kernels: 119 us -> 117 us  [device_step(): pl.pallas_call(kernel, out_shape=(jax.ShapeDtypeStruct(x.shape, x.dtype),...]
where the time goes in v4:
time: 124 us; the launch traced here: 123 us
  Pallas kernels  122 us (98%)
    pallas_call x1, Pallas kernels, device_step(): pl.pallas_call(kernel, out_shape=(jax.ShapeDtypeStruct(x.shape, x.dtype),...  117 us
    pallas_call x1, Pallas kernels, device_step(): pl.pallas_call(place_kernel, out_shape=jax.ShapeDtypeStruct(x.shape, x.dt...  5.25 us

profile of v4, /device:TPU:0, one launch (start us, length us, event | category | flops | bytes accessed | tf_op | source)
XLA Modules:
  0.0 122.6 jit_solution(6386173784538007257)
XLA Ops:
  0.0 117.1 %shard_map.172 = (bf16[512,3072]{1,0:T(8,128)(2,1)}, bf16[512,512]{1,0:T(8,128)(2,1)}) custom-call(s32[4]{0:T(128)} %hot_hbm.1, s32[1,512]{1,0:T(1,128)} %bitcast.37, bf16[512,3072]{1,0:T(8,128)(2,1)} %x_hbm.1, bf16[3072,8192]{1,0:T(8,128)(2,1)} %wg_hbm.1, bf16[3072,8192]{1,0:T(8,128)(2,1)} %wu_hbm.1, bf16[8192,3072]{1,0:T(8,128)(2,1)} %wd_hbm.1, ...), custom_call_target="tpu_custom_call" | custom-call | tf_op jit(solution)/shard_map/pallas_call | solution.py:467
  117.1 5.2 %shard_map.173 = bf16[512,3072]{1,0:T(8,128)(2,1)} custom-call(bf16[512,3072]{1,0:T(8,128)(2,1)} %get-tuple-element.7.y_hbm, bf16[512,512]{1,0:T(8,128)(2,1)} %get-tuple-element.8.unperm_hbm), custom_call_target="tpu_custom_call" | custom-call | tf_op jit(solution)/shard_map/pallas_call | solution.py:505

commit v5 on v4

--- a/solution.py
+++ b/solution.py
@@ -13,7 +13,7 @@
 BF16 = jnp.bfloat16
 
 TN = 512
-FIRST = 8
+FIRST = 9
 
 
 def dot(a, b):
@@ -92,9 +92,9 @@
     own_cols = pl.ds(0, n_own)
     hot_cols = pl.ds(n_own, n_hr)
     hot_group = n_own // 128
-    lead = (FIRST - 1 + n_tiles) % 3
     k_parts = [(k, min(d_model, d_ff - k)) for k in range(0, d_ff, d_model)]
-    assert len(k_parts) == 3 and n_tiles == 2 * FIRST
+    pairs = FIRST - 2
+    assert len(k_parts) == 3 and n_tiles == FIRST + pairs and FIRST % 3 == 0
 
     def cp(src, dst, sem):
         return pltpu.make_async_copy(src, dst, sem)
@@ -120,11 +120,8 @@
             cp(had_hbm.at[:, cols], adbuf.at[ad_slot, hot_cols], ad_sem.at[ad_slot, 1]),
         ]
 
-    def ring(s):
-        return lax.rem(s + FIRST - 1, 3)
-
-    def gu_full(tile, s):
-        return gu_base(tile, ring(s)) + gu_extra(tile, ring(s), lax.rem(s, 4))
+    def gu_full(tile, slot, ad_slot):
+        return gu_base(tile, slot) + gu_extra(tile, slot, ad_slot)
 
     def a_view(i, c, first, size):
         index = i * d_tiles + c
@@ -136,11 +133,11 @@
 
     def down_half(n, i):
         k = lax.rem(n, 3)
-        return jnp.where(k == 0, 6 + i, lax.rem(2 * lead + 3 * (k + 1) + i, 6))
+        return jnp.where(k == 0, 6 + i, 3 * (k - 1) + i)
 
     def down_b(n):
         k = lax.rem(n, 3)
-        return lax.rem(lead + k // 2, 3), lax.rem(k, 2)
+        return k // 2, lax.rem(k, 2)
 
     def down_copies(n, pieces=(0, 1, 2, 3, 4)):
         cols = tile_cols(n)
@@ -249,11 +246,11 @@
 
         @pl.when(s + 3 == FIRST)
         def _():
-            start(gu_extra(FIRST - 1, ahead, 0))
+            start(gu_extra(FIRST - 1, ahead, 2))
 
         @pl.when(s + 2 >= FIRST)
         def _():
-            start(gu_full(jnp.where(s + 2 == FIRST, FIRST, 0), s + 3 - FIRST))
+            start(gu_full(jnp.where(s + 2 == FIRST, FIRST, 0), ahead, jnp.where(s + 2 == FIRST, 3, 0)))
 
         @pl.when(s == 1)
         def _():
@@ -301,39 +298,36 @@
         h[kept, tile_cols(tile)] = act(g[:half], u[:half], dgk, duk)
         h[recv, tile_cols(tile)] = act(g[half:], u[half:], dgr, dur)
 
-    wait(gu_extra(FIRST - 1, (FIRST - 1) % 3, 0))
-    recv_tile(FIRST - 1, (FIRST - 1) % 3, lambda: None)
+    wait(gu_extra(FIRST - 1, 2, 2))
+    recv_tile(FIRST - 1, 2, lambda: None)
+
+    def pair_copies(p):
+        slot = 2 * lax.rem(p, 2)
+        return gu_full(FIRST + p, slot, 3 + lax.rem(p, 2)) + gu_full(p, slot + 1, lax.rem(p, 3))
 
     def second_step(p, carry):
-        s = 2 * p + 1
-        wait(gu_full(FIRST + p, s))
-        start(gu_full(FIRST + p + 1, s + 2))
-
-        @pl.when(p == 1)
-        def _():
+        slot = 2 * lax.rem(p, 2)
+        wait(pair_copies(p))
+
+        @pl.when(p + 1 < pairs)
+        def _():
+            start(pair_copies(p + 1))
+
+        @pl.when(p + 1 == pairs)
+        def _():
+            start(gu_full(pairs, 2, pairs % 3))
             start(down_copies(0, (0, 1, 2)))
 
-        all_tile(FIRST + p, ring(s), lambda: add_low(jnp.where(p == 0, FIRST - 1, p - 1), lax.rem(s + 3, 4)))
-        wait(gu_full(p, s + 1))
-
-        @pl.when(p + 2 < FIRST)
-        def _():
-            start(gu_full(p + 1, s + 3))
-
-        @pl.when(p + 2 == FIRST)
-        def _():
-            start(down_copies(0, (3, 4)) + down_copies(1, (0, 1, 3, 4)))
-
-        recv_tile(p, ring(s + 1), lambda: add_low(FIRST + p, lax.rem(s, 4)))
+        all_tile(FIRST + p, slot, lambda: add_low(jnp.where(p == 0, FIRST - 1, p - 1), lax.rem(p + 2, 3)))
+        recv_tile(p, slot + 1, lambda: add_low(FIRST + p, 3 + lax.rem(p, 2)))
         return carry
 
-    lax.fori_loop(0, FIRST - 1, second_step, 0)
-    s_last = n_tiles - 1
-    wait(gu_full(n_tiles - 1, s_last))
-    start(down_copies(1, (2,)) + down_copies(2, (0, 3, 4)))
-    all_tile(n_tiles - 1, (s_last + FIRST - 1) % 3, lambda: add_low(FIRST - 2, (s_last + 3) % 4))
+    lax.fori_loop(0, pairs, second_step, 0)
+    wait(gu_full(pairs, 2, pairs % 3))
+    start(down_copies(0, (3, 4)) + down_copies(1) + down_copies(2, (0, 3, 4)))
+    recv_tile(pairs, 2, lambda: add_low(pairs - 1, (pairs - 1) % 3))
     start(down_copies(2, (1, 2)))
-    add_low(n_tiles - 1, (n_tiles - 1) % 4)
+    add_low(pairs, pairs % 3)
 
     pdm[kept, hot_cols] = masked_bf16(pd[kept, hot_cols], cls_kept, hot_group)
     pdm[recv, :] = masked_bf16(pd[recv, :], cls_recv, 0)
@@ -481,14 +475,14 @@
                 pltpu.VMEM((tokens, n_all), F32),
                 pltpu.VMEM((tokens, n_all), BF16),
                 pltpu.VMEM((9, d_model, TN), BF16),
-                pltpu.VMEM((3, 2, n_all, TN), BF16),
-                pltpu.VMEM((4, n_all, TN), BF16),
+                pltpu.VMEM((4, 2, n_all, TN), BF16),
+                pltpu.VMEM((5, n_all, TN), BF16),
                 pltpu.VMEM((tokens, tokens), BF16),
                 pltpu.SemaphoreType.DMA((2,)),
                 pltpu.SemaphoreType.DMA((d_tiles,)),
                 pltpu.SemaphoreType.DMA((4, d_tiles)),
-                pltpu.SemaphoreType.DMA((3, 6)),
-                pltpu.SemaphoreType.DMA((4, 2)),
+                pltpu.SemaphoreType.DMA((4, 6)),
+                pltpu.SemaphoreType.DMA((5, 2)),
                 pltpu.SemaphoreType.DMA((3, 5)),
                 pltpu.SemaphoreType.DMA((d_tiles, 2)),
                 pltpu.SemaphoreType.DMA,

time: 124 us -> 122 us (0.984)
  no operation moved by 1% of the time
where the time goes in v5:
time: 122 us
  Pallas kernels  121 us (99%)
    pallas_call x1, Pallas kernels, device_step(): pl.pallas_call(kernel, out_shape=(jax.ShapeDtypeStruct(x.shape, x.dtype),...  116 us
    pallas_call x1, Pallas kernels, device_step(): pl.pallas_call(place_kernel, out_shape=jax.ShapeDtypeStruct(x.shape, x.dt...  5.25 us

profile of v5, /device:TPU:0, one launch (start us, length us, event | category | flops | bytes accessed | tf_op | source)
XLA Modules:
  0.0 121.6 jit_solution(9524755437642997850)
XLA Ops:
  0.0 116.2 %shard_map.172 = (bf16[512,3072]{1,0:T(8,128)(2,1)}, bf16[512,512]{1,0:T(8,128)(2,1)}) custom-call(s32[4]{0:T(128)} %hot_hbm.1, s32[1,512]{1,0:T(1,128)} %bitcast.37, bf16[512,3072]{1,0:T(8,128)(2,1)} %x_hbm.1, bf16[3072,8192]{1,0:T(8,128)(2,1)} %wg_hbm.1, bf16[3072,8192]{1,0:T(8,128)(2,1)} %wu_hbm.1, bf16[8192,3072]{1,0:T(8,128)(2,1)} %wd_hbm.1, ...), custom_call_target="tpu_custom_call" | custom-call | tf_op jit(solution)/shard_map/pallas_call | solution.py:461
  116.2 5.2 %shard_map.173 = bf16[512,3072]{1,0:T(8,128)(2,1)} custom-call(bf16[512,3072]{1,0:T(8,128)(2,1)} %get-tuple-element.7.y_hbm, bf16[512,512]{1,0:T(8,128)(2,1)} %get-tuple-element.8.unperm_hbm), custom_call_target="tpu_custom_call" | custom-call | tf_op jit(solution)/shard_map/pallas_call | solution.py:499

commit v6 on v5

--- a/solution.py
+++ b/solution.py
@@ -94,6 +94,7 @@
     hot_group = n_own // 128
     k_parts = [(k, min(d_model, d_ff - k)) for k in range(0, d_ff, d_model)]
     pairs = FIRST - 2
+    assert 2 * n_hr == d_model // 6 and n_own == 2 * n_hr
     assert len(k_parts) == 3 and n_tiles == FIRST + pairs and FIRST % 3 == 0
 
     def cp(src, dst, sem):
@@ -106,19 +107,31 @@
         cols = tile_cols(tile)
         return [
             cp(wg_hbm.at[:, cols], wbuf.at[2 * slot], w_sem.at[slot, 0]),
-            cp(wu_hbm.at[:, cols], wbuf.at[2 * slot + 1], w_sem.at[slot, 1]),
-            cp(hbg_hbm.at[:, cols], bbuf.at[slot, 0, hot_cols], w_sem.at[slot, 2]),
-            cp(hbu_hbm.at[:, cols], bbuf.at[slot, 1, hot_cols], w_sem.at[slot, 3]),
+            cp(wu_hbm.at[:, cols], wbuf.at[2 * slot + 1], w_sem.at[slot, 0]),
+            cp(hbg_hbm.at[:, cols], bbuf.at[slot, 0, hot_cols], w_sem.at[slot, 1]),
+            cp(hbu_hbm.at[:, cols], bbuf.at[slot, 1, hot_cols], w_sem.at[slot, 1]),
         ]
 
     def gu_extra(tile, slot, ad_slot):
         cols = tile_cols(tile)
         return [
-            cp(bg_hbm.at[:, cols], bbuf.at[slot, 0, own_cols], w_sem.at[slot, 4]),
-            cp(bu_hbm.at[:, cols], bbuf.at[slot, 1, own_cols], w_sem.at[slot, 5]),
-            cp(ad_hbm.at[:, cols], adbuf.at[ad_slot, own_cols], ad_sem.at[ad_slot, 0]),
-            cp(had_hbm.at[:, cols], adbuf.at[ad_slot, hot_cols], ad_sem.at[ad_slot, 1]),
+            cp(bg_hbm.at[:, cols], bbuf.at[slot, 0, own_cols], w_sem.at[slot, 2]),
+            cp(bu_hbm.at[:, cols], bbuf.at[slot, 1, own_cols], w_sem.at[slot, 2]),
+            cp(ad_hbm.at[:, cols], adbuf.at[ad_slot, own_cols], ad_sem.at[ad_slot]),
+            cp(had_hbm.at[:, cols], adbuf.at[ad_slot, hot_cols], ad_sem.at[ad_slot]),
         ]
+
+    def whole(ref, sem):
+        return cp(ref, ref, sem)
+
+    def base_done(slot):
+        return [whole(wbuf.at[pl.ds(2 * slot, 2)], w_sem.at[slot, 0]), whole(bbuf.at[slot, :, hot_cols], w_sem.at[slot, 1])]
+
+    def extra_done(slot, ad_slot):
+        return [whole(bbuf.at[slot, :, own_cols], w_sem.at[slot, 2]), whole(adbuf.at[ad_slot], ad_sem.at[ad_slot])]
+
+    def full_done(slot, ad_slot):
+        return base_done(slot) + extra_done(slot, ad_slot)
 
     def gu_full(tile, slot, ad_slot):
         return gu_base(tile, slot) + gu_extra(tile, slot, ad_slot)
@@ -129,7 +142,7 @@
         return wbuf.at[6 + index // per, pl.ds((index % per) * n_all + first, size)]
 
     def a_copies(i, src, first, size, side):
-        return [cp(src.at[:, pl.ds(c * TN, TN)], a_view(i, c, first, size), at_sem.at[2 * side + i, c]) for c in range(d_tiles)]
+        return [cp(src.at[:, pl.ds(c * TN, TN)], a_view(i, c, first, size), at_sem.at[side]) for c in range(d_tiles)]
 
     def down_half(n, i):
         k = lax.rem(n, 3)
@@ -162,7 +175,7 @@
             c.wait()
 
     id_copies = [cp(ids_hbm, ids, id_sem.at[0]), cp(hot_hbm, hot_ids, id_sem.at[1])]
-    x_copies = [cp(x_hbm.at[:, pl.ds(n * TN, TN)], xy.at[n], x_sem.at[n]) for n in range(d_tiles)]
+    x_copies = [cp(x_hbm.at[:, pl.ds(n * TN, TN)], xy.at[n], x_sem) for n in range(d_tiles)]
     a_hot = a_copies(0, hag_hbm, n_own, n_hr, 0) + a_copies(1, hau_hbm, n_own, n_hr, 0)
     a_own = a_copies(0, ag_hbm, 0, n_own, 1) + a_copies(1, au_hbm, 0, n_own, 1)
     start(id_copies)
@@ -183,7 +196,7 @@
     cls_rows = dot_t(perm, jnp.broadcast_to(cls, (128, tokens)).astype(BF16)).astype(BF16)
     xsend[:, pl.ds(d_model, 128)] = cls_rows[half:]
     xa[kept, pl.ds(d_model, 128)] = cls_rows[:half]
-    wait(x_copies)
+    wait([whole(xy, x_sem)])
     for n in range(d_tiles):
         xsend[:, pl.ds(n * TN, TN)] = dot(perm[half:], xy[n]).astype(BF16)
 
@@ -206,7 +219,7 @@
         x_remote(d).start()
     for n in range(d_tiles):
         xa[kept, pl.ds(n * TN, TN)] = dot(perm[:half], xy[n]).astype(BF16)
-    wait(a_hot)
+    wait([whole(wbuf.at[6], at_sem.at[0])])
     xa[my_rows, :] = xsend[my_block, :]
     pos_col = jnp.transpose(jnp.broadcast_to(pos, (128, tokens)))[:, 0:1].astype(jnp.int32)
     unperm[...] = (pos_col == lax.broadcasted_iota(jnp.int32, (tokens, tokens), 1)).astype(BF16)
@@ -238,7 +251,7 @@
     def first_step(s, carry):
         slot = lax.rem(s, 3)
         ahead = lax.rem(s + 2, 3)
-        wait(gu_base(s, slot))
+        wait(base_done(slot))
 
         @pl.when(s + 2 < FIRST)
         def _():
@@ -247,14 +260,11 @@
         @pl.when(s + 3 == FIRST)
         def _():
             start(gu_extra(FIRST - 1, ahead, 2))
+            start(a_own)
 
         @pl.when(s + 2 >= FIRST)
         def _():
             start(gu_full(jnp.where(s + 2 == FIRST, FIRST, 0), ahead, jnp.where(s + 2 == FIRST, 3, 0)))
-
-        @pl.when(s == 1)
-        def _():
-            start(a_own)
 
         xk = xa[kept, pl.ds(0, d_model)]
         dg = delta(pg[kept, hot_cols], bbuf[slot, 0, hot_cols, :])
@@ -265,7 +275,7 @@
     lax.fori_loop(0, FIRST, first_step, 0)
 
     cp(unperm, unperm_hbm, p_sem).start()
-    wait(a_own)
+    wait([whole(wbuf.at[pl.ds(6, 2)], at_sem.at[1])])
     x_all.wait_recv()
     cls_recv = xa[recv, pl.ds(d_model, 128)].astype(F32)
     low_g, low_u = low_rank(recv, 0, n_all)
@@ -298,7 +308,7 @@
         h[kept, tile_cols(tile)] = act(g[:half], u[:half], dgk, duk)
         h[recv, tile_cols(tile)] = act(g[half:], u[half:], dgr, dur)
 
-    wait(gu_extra(FIRST - 1, 2, 2))
+    wait(extra_done(2, 2))
     recv_tile(FIRST - 1, 2, lambda: None)
 
     def pair_copies(p):
@@ -307,7 +317,7 @@
 
     def second_step(p, carry):
         slot = 2 * lax.rem(p, 2)
-        wait(pair_copies(p))
+        wait(full_done(slot, 3 + lax.rem(p, 2)) + full_done(slot + 1, lax.rem(p, 3)))
 
         @pl.when(p + 1 < pairs)
         def _():
@@ -323,7 +333,7 @@
         return carry
 
     lax.fori_loop(0, pairs, second_step, 0)
-    wait(gu_full(pairs, 2, pairs % 3))
+    wait(full_done(2, pairs % 3))
     start(down_copies(0, (3, 4)) + down_copies(1) + down_copies(2, (0, 3, 4)))
     recv_tile(pairs, 2, lambda: add_low(pairs - 1, (pairs - 1) % 3))
     start(down_copies(2, (1, 2)))
@@ -391,13 +401,11 @@
         send_back(n)
         return carry
 
-    def late_kept(n, carry):
+    lax.fori_loop(early, d_tiles, late_recv, 0)
+    for n in range(early, d_tiles):
         down_kept(n)
+    for n in range(early, d_tiles):
         start(y_local(n))
-        return carry
-
-    lax.fori_loop(early, d_tiles, late_recv, 0)
-    lax.fori_loop(early, d_tiles, late_kept, 0)
 
     x_all.wait_send()
     cp(unperm, unperm_hbm, p_sem).wait()
@@ -421,7 +429,7 @@
     for n in range(tiles):
         y_copy(n).start()
     p_copy.wait()
-    for group in ((0,), (1, 2), tuple(range(3, tiles))):
+    for group in ((0,), tuple(range(1, tiles - 2)), (tiles - 2, tiles - 1)):
         for n in group:
             y_copy(n).wait()
         for n in group:
@@ -479,10 +487,10 @@
                 pltpu.VMEM((5, n_all, TN), BF16),
                 pltpu.VMEM((tokens, tokens), BF16),
                 pltpu.SemaphoreType.DMA((2,)),
-                pltpu.SemaphoreType.DMA((d_tiles,)),
-                pltpu.SemaphoreType.DMA((4, d_tiles)),
-                pltpu.SemaphoreType.DMA((4, 6)),
-                pltpu.SemaphoreType.DMA((5, 2)),
+                pltpu.SemaphoreType.DMA,
+                pltpu.SemaphoreType.DMA((2,)),
+                pltpu.SemaphoreType.DMA((4, 3)),
+                pltpu.SemaphoreType.DMA((5,)),
                 pltpu.SemaphoreType.DMA((3, 5)),
                 pltpu.SemaphoreType.DMA((d_tiles, 2)),
                 pltpu.SemaphoreType.DMA,

time: 122 us -> 120 us (0.984)
  no operation moved by 1% of the time
where the time goes in v6:
time: 120 us
  Pallas kernels  120 us (100%)
    pallas_call x1, Pallas kernels, device_step(): pl.pallas_call(kernel, out_shape=(jax.ShapeDtypeStruct(x.shape, x.dtype),...  115 us
    pallas_call x1, Pallas kernels, device_step(): pl.pallas_call(place_kernel, out_shape=jax.ShapeDtypeStruct(x.shape, x.dt...  5.08 us

profile of v6, /device:TPU:0, one launch (start us, length us, event | category | flops | bytes accessed | tf_op | source)
XLA Modules:
  0.0 120.3 jit_solution(14078463017895422811)
XLA Ops:
  0.0 115.0 %shard_map.172 = (bf16[512,3072]{1,0:T(8,128)(2,1)}, bf16[512,512]{1,0:T(8,128)(2,1)}) custom-call(s32[4]{0:T(128)} %hot_hbm.1, s32[1,512]{1,0:T(1,128)} %bitcast.37, bf16[512,3072]{1,0:T(8,128)(2,1)} %x_hbm.1, bf16[3072,8192]{1,0:T(8,128)(2,1)} %wg_hbm.1, bf16[3072,8192]{1,0:T(8,128)(2,1)} %wu_hbm.1, bf16[8192,3072]{1,0:T(8,128)(2,1)} %wd_hbm.1, ...), custom_call_target="tpu_custom_call" | custom-call | tf_op jit(solution)/shard_map/pallas_call | solution.py:469
  115.0 5.1 %shard_map.173 = bf16[512,3072]{1,0:T(8,128)(2,1)} custom-call(bf16[512,3072]{1,0:T(8,128)(2,1)} %get-tuple-element.7.y_hbm, bf16[512,512]{1,0:T(8,128)(2,1)} %get-tuple-element.8.unperm_hbm), custom_call_target="tpu_custom_call" | custom-call | tf_op jit(solution)/shard_map/pallas_call | solution.py:507

commit v7 on v6

--- a/solution.py
+++ b/solution.py
@@ -76,7 +76,7 @@
                hag_hbm, hbg_hbm, hau_hbm, hbu_hbm, had_hbm, hbd_hbm,
                y_hbm, unperm_hbm,
                hot_ids, ids, xy, xsend, xa, h, pg, pu, pd, pdm, wbuf, bbuf, adbuf, unperm,
-               id_sem, x_sem, at_sem, w_sem, ad_sem, d_sem, y_sem, p_sem, s1, r1, s2, r2):
+               id_sem, x_sem, self_sem, at_sem, w_sem, ad_sem, d_sem, y_sem, p_sem, s1, r1, s2, r2):
     me = lax.axis_index("data")
     tokens, d_model = x_hbm.shape
     d_ff = wg_hbm.shape[1]
@@ -217,10 +217,11 @@
 
     for d in range(1, group):
         x_remote(d).start()
+    x_self = cp(xsend.at[my_block], xa.at[my_rows], self_sem)
+    x_self.start()
+    wait([whole(wbuf.at[6], at_sem.at[0])])
     for n in range(d_tiles):
         xa[kept, pl.ds(n * TN, TN)] = dot(perm[:half], xy[n]).astype(BF16)
-    wait([whole(wbuf.at[6], at_sem.at[0])])
-    xa[my_rows, :] = xsend[my_block, :]
     pos_col = jnp.transpose(jnp.broadcast_to(pos, (128, tokens)))[:, 0:1].astype(jnp.int32)
     unperm[...] = (pos_col == lax.broadcasted_iota(jnp.int32, (tokens, tokens), 1)).astype(BF16)
 
@@ -275,13 +276,15 @@
     lax.fori_loop(0, FIRST, first_step, 0)
 
     cp(unperm, unperm_hbm, p_sem).start()
+    wait(extra_done(2, 2))
+    x_self.wait()
     wait([whole(wbuf.at[pl.ds(6, 2)], at_sem.at[1])])
     x_all.wait_recv()
+    pd[...] = jnp.zeros_like(pd)
     cls_recv = xa[recv, pl.ds(d_model, 128)].astype(F32)
     low_g, low_u = low_rank(recv, 0, n_all)
     pg[recv, :] = masked_bf16(low_g, cls_recv, 0)
     pu[recv, :] = masked_bf16(low_u, cls_recv, 0)
-    pd[...] = jnp.zeros_like(pd)
 
     def add_low(tile, ad_slot):
         cols = tile_cols(tile)
@@ -292,8 +295,8 @@
 
     def recv_tile(tile, slot, between):
         xr = xa[recv, pl.ds(0, d_model)]
+        g, u = dot(xr, wbuf[2 * slot]), dot(xr, wbuf[2 * slot + 1])
         dg, du = delta(pg[recv, :], bbuf[slot, 0]), delta(pu[recv, :], bbuf[slot, 1])
-        g, u = dot(xr, wbuf[2 * slot]), dot(xr, wbuf[2 * slot + 1])
         between()
         h[recv, tile_cols(tile)] = act(g, u, dg, du)
 
@@ -308,7 +311,6 @@
         h[kept, tile_cols(tile)] = act(g[:half], u[:half], dgk, duk)
         h[recv, tile_cols(tile)] = act(g[half:], u[half:], dgr, dur)
 
-    wait(extra_done(2, 2))
     recv_tile(FIRST - 1, 2, lambda: None)
 
     def pair_copies(p):
@@ -487,6 +489,7 @@
                 pltpu.VMEM((5, n_all, TN), BF16),
                 pltpu.VMEM((tokens, tokens), BF16),
                 pltpu.SemaphoreType.DMA((2,)),
+                pltpu.SemaphoreType.DMA,
                 pltpu.SemaphoreType.DMA,
                 pltpu.SemaphoreType.DMA((2,)),
                 pltpu.SemaphoreType.DMA((4, 3)),

time: 120 us -> 120 us (level)
  no operation moved by 1% of the time
where the time goes in v7:
time: 120 us
  Pallas kernels  120 us (100%)
    pallas_call x1, Pallas kernels, device_step(): pl.pallas_call(kernel, out_shape=(jax.ShapeDtypeStruct(x.shape, x.dtype),...  115 us
    pallas_call x1, Pallas kernels, device_step(): pl.pallas_call(place_kernel, out_shape=jax.ShapeDtypeStruct(x.shape, x.dt...  5.08 us

profile of v7, /device:TPU:0, one launch (start us, length us, event | category | flops | bytes accessed | tf_op | source)
XLA Modules:
  0.0 120.2 jit_solution(12835590744521068096)
XLA Ops:
  0.0 115.0 %shard_map.172 = (bf16[512,3072]{1,0:T(8,128)(2,1)}, bf16[512,512]{1,0:T(8,128)(2,1)}) custom-call(s32[4]{0:T(128)} %hot_hbm.1, s32[1,512]{1,0:T(1,128)} %bitcast.37, bf16[512,3072]{1,0:T(8,128)(2,1)} %x_hbm.1, bf16[3072,8192]{1,0:T(8,128)(2,1)} %wg_hbm.1, bf16[3072,8192]{1,0:T(8,128)(2,1)} %wu_hbm.1, bf16[8192,3072]{1,0:T(8,128)(2,1)} %wd_hbm.1, ...), custom_call_target="tpu_custom_call" | custom-call | tf_op jit(solution)/shard_map/pallas_call | solution.py:471
  115.0 5.1 %shard_map.173 = bf16[512,3072]{1,0:T(8,128)(2,1)} custom-call(bf16[512,3072]{1,0:T(8,128)(2,1)} %get-tuple-element.7.y_hbm, bf16[512,512]{1,0:T(8,128)(2,1)} %get-tuple-element.8.unperm_hbm), custom_call_target="tpu_custom_call" | custom-call | tf_op jit(solution)/shard_map/pallas_call | solution.py:510
